TPU v7x, 32 devices: a whole 2x2x4 slice. The times are simulated.
32 devices in a mesh: px: 2 (over x), py: 16 (over z, y, core).
Axes of the slice: x: 2, y: 2, z: 4, core: 2. Of those that a mesh axis runs over, the one named last changes fastest.
Arguments:
- populations: float32 [19, 2, 256, 512], P(None, None, ('py', 'px')), may hold values from 0.02 to 0.12
- pore: int32 [2, 256, 512], P(None, ('py', 'px')), may hold values 0 or 1
Outputs:
- flow: float32 [19, 2, 256, 512], P(None, None, 'py', 'px')
All inputs are finite; a program needn't handle non-finite values. No bound on the sum of `pore` on one device may be relied on, other than what follows from the above.
Results may differ from a plain program's by a relative error of at most 0.0001.
Values sent between devices are 32-bit elements; how exact they have to be, the bound alone decides.
A program may use at most 128 MiB of HBM per device.

v0:
```python
import functools

import jax
import jax.numpy as jnp
from jax import lax
from jax.experimental import pallas as pl
from jax.experimental.pallas import tpu as pltpu
from jax.sharding import PartitionSpec as P

STEPS = 2
MESH = pl.DeviceIdType.MESH

lattice_velocity = [
    (0, 0, 0),
    (1, 0, 0),
    (-1, 0, 0),
    (0, 1, 0),
    (0, -1, 0),
    (0, 0, 1),
    (0, 0, -1),
    (1, 1, 0),
    (-1, -1, 0),
    (1, -1, 0),
    (-1, 1, 0),
    (1, 0, 1),
    (-1, 0, -1),
    (1, 0, -1),
    (-1, 0, 1),
    (0, 1, 1),
    (0, -1, -1),
    (0, 1, -1),
    (0, -1, 1),
]
lattice_weights = [1.0 / 3.0] + [1.0 / 18.0] * 6 + [1.0 / 36.0] * 12
opposite = [0, 2, 1, 4, 3, 6, 5, 8, 7, 10, 9, 12, 11, 14, 13, 16, 15, 18, 17]
relax_time = 0.8
body_force = 0.005

Q = len(lattice_velocity)
LANES = 128
ROWS = 8
HALO = 2
VMEM_LIMIT = 24 * 1024 * 1024
SOLID = -3.0e38


def collide_tile(fields, fluid):
    keep = 1.0 - 1.0 / relax_time
    gain = 1.0 / relax_time
    is_open = fluid > 0.5
    density = functools.reduce(lambda x, y: x + y, fields)
    density = jnp.where(is_open, density, 1.0)
    inverse = 1.0 / density
    vel = []
    for column in range(3):
        plus = [fields[s] for s in range(Q) if lattice_velocity[s][column] > 0]
        minus = [fields[s] for s in range(Q) if lattice_velocity[s][column] < 0]
        total = functools.reduce(lambda x, y: x + y, plus) - functools.reduce(lambda x, y: x + y, minus)
        vel.append(total * inverse)
    vel[2] = vel[2] + relax_time * body_force
    speed = vel[0] * vel[0] + vel[1] * vel[1] + vel[2] * vel[2]
    base = 1.0 - 1.5 * speed
    result = [None] * Q
    scaled = {w: density * (gain * w) for w in sorted(set(lattice_weights))}
    result[0] = jnp.where(is_open, keep * fields[0] + scaled[lattice_weights[0]] * base, SOLID)
    for slot in range(1, Q, 2):
        other = opposite[slot]
        along = None
        for column in range(3):
            sign = lattice_velocity[slot][column]
            if sign == 0:
                continue
            term = vel[column]
            if along is None:
                along = term if sign > 0 else -term
            else:
                along = along + term if sign > 0 else along - term
        weight = scaled[lattice_weights[slot]]
        triple = 3.0 * along
        even = weight * (base + 0.5 * triple * triple)
        odd = weight * triple
        result[slot] = jnp.where(is_open, keep * fields[slot] + (even + odd), SOLID)
        result[other] = jnp.where(is_open, keep * fields[other] + (even - odd), SOLID)
    return result


def kernel(
    across, along, pop_ref, pore_ref, post, mask,
    cells, strip, voxels, packs, edges,
    local_sem, a_send, a_recv, b_send, b_recv, e_send, e_recv, h_send, h_recv,
):
    _, planes, rows, _ = pop_ref.shape
    height = across * rows
    width = pop_ref.shape[3] // across
    tall = height + ROWS
    wide = width + LANES
    groups = edges.shape[0]
    per_group = LANES // 4
    me = lax.axis_index("px")
    here = lax.axis_index("py")
    up = lax.rem(here + along - 1, along)
    down = lax.rem(here + 1, along)

    own_rows = pl.ds(pl.multiple_of(me * rows, rows), rows)
    own_cols = pl.ds(pl.multiple_of(me * width, width), width)
    load_pore = pltpu.make_async_copy(pore_ref, voxels, local_sem.at[0])
    load_own = pltpu.make_async_copy(
        pop_ref.at[:, :, :, own_cols], cells.at[0:Q, :, own_rows, 0:width], local_sem.at[1]
    )
    load_strip = []
    for step in range(1, across + 1):
        cols = pl.ds(pl.multiple_of(lax.rem(me + step, across) * width, width), width)
        load_strip.append(
            pltpu.make_async_copy(
                pop_ref.at[:, :, :, cols], strip.at[0:Q, :, :, cols], local_sem.at[1 + step]
            )
        )
    load_pore.start()
    for copy in load_strip:
        copy.start()
    load_own.start()

    barrier = pltpu.get_barrier_semaphore()
    for step in range(1, across):
        pl.semaphore_signal(barrier, inc=1, device_id=(lax.rem(me + step, across), here), device_id_type=MESH)
    for to in (up, down):
        pl.semaphore_signal(barrier, inc=1, device_id=(me, to), device_id_type=MESH)

    load_pore.wait()
    strip[Q] = voxels[...].astype(jnp.float32)
    for copy in load_strip[:-1]:
        copy.wait()
    pl.semaphore_wait(barrier, across - 1 + 2)

    def near(source):
        return (rows - HALO, rows) if source == across - 1 else (0, HALO)

    def far(source):
        return (0, rows - HALO) if source == across - 1 else (HALO, rows)

    def strip_copy(source, target, part, cols, send, recv):
        low, high = part(source)
        start = target * width
        return pltpu.make_async_remote_copy(
            src_ref=strip.at[:, :, low:high, start + cols[0] : start + cols[1]],
            dst_ref=cells.at[:, :, source * rows + low : source * rows + high, cols[0] : cols[1]],
            send_sem=send,
            recv_sem=recv,
            device_id=(target, here),
            device_id_type=MESH,
        )

    def near_copy(source, target):
        return strip_copy(source, target, near, (0, width), a_send.at[target], a_recv.at[source])

    pieces = [(col, col + LANES) for col in range(0, width, LANES)]

    def far_copies(source, target):
        return [
            strip_copy(source, target, far, cols, b_send.at[target, n], b_recv.at[source, n])
            for n, cols in enumerate(pieces)
        ]

    def edge_copy(source, target):
        return pltpu.make_async_remote_copy(
            src_ref=packs.at[target],
            dst_ref=edges.at[:, source * rows : (source + 1) * rows, :],
            send_sem=e_send.at[target],
            recv_sem=e_recv.at[source],
            device_id=(target, here),
            device_id_type=MESH,
        )

    def halo_copies(way):
        if way == 0:
            source, dest, to = 0, height, up
        else:
            source, dest, to = height - HALO, tall - HALO, down
        return [
            pltpu.make_async_remote_copy(
                src_ref=cells.at[:, :, source : source + HALO, 0:width],
                dst_ref=cells.at[:, :, dest : dest + HALO, 0:width],
                send_sem=h_send.at[2 * way],
                recv_sem=h_recv.at[2 * way],
                device_id=(me, to),
                device_id_type=MESH,
            ),
            pltpu.make_async_remote_copy(
                src_ref=edges.at[:, source : source + HALO, :],
                dst_ref=edges.at[:, dest : dest + HALO, :],
                send_sem=h_send.at[2 * way + 1],
                recv_sem=h_recv.at[2 * way + 1],
                device_id=(me, to),
                device_id_type=MESH,
            ),
        ]

    def peers(mine):
        return [(mine + step) % across for step in range(1, across)]

    def on_each(action):
        for mine in range(across):
            pl.when(me == mine)(functools.partial(action, mine))

    def send_near(mine):
        for target in peers(mine):
            near_copy(mine, target).start()

    on_each(send_near)
    load_strip[-1].wait()

    lane = lax.broadcasted_iota(jnp.int32, (rows, LANES), 1)
    total = across * width
    for target in range(across):
        first = (target + 1) * width % total
        last = (target * width - LANES) % total
        for group in range(groups):
            packed = jnp.zeros((rows, LANES), jnp.float32)
            for place in range(per_group):
                slab = group * per_group + place
                if slab >= (Q + 1) * planes:
                    break
                field, plane = slab // planes, slab % planes
                edge = jnp.where(
                    lane < LANES // 2,
                    strip[field, plane, :, first : first + LANES],
                    strip[field, plane, :, last : last + LANES],
                )
                if place == 0:
                    packed = edge
                else:
                    moved = pltpu.roll(edge, 4 * place, 1)
                    packed = jnp.where((lane >= 4 * place - 2) & (lane < 4 * place + 2), moved, packed)
            packs[target, group] = packed

    ends = ((0, 0), (across - 1, 1))

    def send_rest(mine):
        for target in peers(mine):
            edge_copy(mine, target).start()
        for target in peers(mine):
            for copy in far_copies(mine, target):
                copy.start()

    on_each(send_rest)
    edges[:, own_rows, :] = packs[me]
    cells[Q, :, own_rows, 0:width] = voxels[:, :, own_cols].astype(jnp.float32)
    load_own.wait()

    def unpack(tile):
        at = pl.ds(pl.multiple_of(tile * ROWS, ROWS), ROWS)
        for slab in range((Q + 1) * planes):
            group, place = slab // per_group, slab % per_group
            packed = edges[group, at, :]
            moved = pltpu.roll(packed, LANES - 4 * place, 1) if place else packed
            cells[slab // planes, slab % planes, at, width:wide] = moved

    def collide(tile, columns):
        at = pl.ds(pl.multiple_of(tile * ROWS, ROWS), ROWS)
        for plane in range(planes):
            for col in columns:
                fields = [cells[slot, plane, at, col : col + LANES] for slot in range(Q)]
                result = collide_tile(fields, cells[Q, plane, at, col : col + LANES])
                for slot in range(Q):
                    post[slot, plane, at, col : col + LANES] = result[slot]

    tiles = tall // ROWS
    per_strip = rows // ROWS
    all_columns = range(0, wide, LANES)

    def relay_own(mine):
        for source, way in ends:
            if source == mine:
                for copy in halo_copies(way):
                    copy.start()

    on_each(relay_own)
    for part in range(per_strip):
        unpack(me * per_strip + part)
        collide(me * per_strip + part, all_columns)

    def relay(mine):
        for source, way in ends:
            if source != mine:
                near_copy(source, mine).wait_recv()
                edge_copy(source, mine).wait_recv()
                for copy in halo_copies(way):
                    copy.start()
        for source in peers(mine):
            if source not in (0, across - 1):
                near_copy(source, mine).wait_recv()
                edge_copy(source, mine).wait_recv()

    on_each(relay)

    def source_at(step):
        return lax.rem(me + step, across)

    def take_piece(step, n):
        source = source_at(step)
        low, high = pieces[n]
        arrived = cells.at[:, :, 0 : rows - HALO, low:high]
        pltpu.make_async_copy(arrived, arrived, b_recv.at[source, n]).wait()
        for part in range(per_strip):
            collide(source * per_strip + part, (low,))

    def take_edges(step, carry):
        for part in range(per_strip):
            unpack(source_at(step) * per_strip + part)
            collide(source_at(step) * per_strip + part, (width,))
        return carry

    def take_most(step, carry):
        for n in range(len(pieces) - 1):
            take_piece(step, n)
        return carry

    def take_last(step, carry):
        take_piece(step, len(pieces) - 1)
        return carry

    lax.fori_loop(1, across, take_edges, 0)
    lax.fori_loop(1, across, take_most, 0)
    for way in range(2):
        for copy in halo_copies(way):
            copy.wait_recv()
    unpack(tiles - 1)
    collide(tiles - 1, all_columns)
    lax.fori_loop(1, across, take_last, 0)

    def sent(mine):
        for target in peers(mine):
            near_copy(mine, target).wait_send()
            edge_copy(mine, target).wait_send()
            for copy in far_copies(mine, target):
                copy.wait_send()
        for way in range(2):
            for copy in halo_copies(way):
                copy.wait_send()

    on_each(sent)

    def collide_all(tile, carry):
        collide(tile, all_columns)
        return carry

    for step in range(STEPS):
        if step:
            lax.fori_loop(0, tiles, collide_all, 0)
        if step < STEPS - 1:
            for plane in range(planes):
                is_open = cells[Q, plane] > 0.5
                for slot in range(Q):
                    cells[slot, plane] = streamed(post, is_open, slot, plane)
    mask[...] = cells[Q]


def streamed(post, is_open, slot, plane):
    _, planes, tall, wide = post.shape
    vector = lattice_velocity[slot]
    value = post[slot, (plane - vector[2]) % planes]
    if vector[1]:
        value = pltpu.roll(value, vector[1] % tall, 0)
    if vector[0]:
        value = pltpu.roll(value, vector[0] % wide, 1)
    if slot:
        value = jnp.where(value != SOLID, value, post[opposite[slot], plane])
    return jnp.where(is_open, value, 0.0)


def finish(post, mask, out_ref, flow, sems):
    _, planes, height, width = flow.shape
    copies = []
    for slot in range(Q):
        for plane in range(planes):
            value = streamed(post, mask[plane] > 0.5, slot, plane)
            flow[slot, plane] = value[:height, :width]
        copies.append(pltpu.make_async_copy(flow.at[slot], out_ref.at[slot], sems.at[slot]))
        if slot:
            copies[slot - 1].start()
    copies[-1].start()
    for copy in copies:
        copy.wait()


def body(across, along, populations, pore):
    count, planes, rows, columns = populations.shape
    height = across * rows
    width = columns // across
    tall = height + ROWS
    wide = width + LANES
    groups = -(-(count + 1) * planes * 4 // LANES)
    post, mask = pl.pallas_call(
        functools.partial(kernel, across, along),
        out_shape=(
            pltpu.VMEM((count, planes, tall, wide), jnp.float32),
            pltpu.VMEM((planes, tall, wide), jnp.float32),
        ),
        in_specs=[pl.BlockSpec(memory_space=pltpu.HBM)] * 2,
        out_specs=[pl.BlockSpec(memory_space=pltpu.VMEM)] * 2,
        scratch_shapes=[
            pltpu.VMEM((count + 1, planes, tall, wide), jnp.float32),
            pltpu.VMEM((count + 1, planes, rows, columns), jnp.float32),
            pltpu.VMEM((planes, rows, columns), jnp.int32),
            pltpu.VMEM((across, groups, rows, LANES), jnp.float32),
            pltpu.VMEM((groups, tall, LANES), jnp.float32),
            pltpu.SemaphoreType.DMA((2 + across,)),
            pltpu.SemaphoreType.DMA((across,)),
            pltpu.SemaphoreType.DMA((across,)),
            pltpu.SemaphoreType.DMA((across, width // LANES)),
            pltpu.SemaphoreType.DMA((across, width // LANES)),
            pltpu.SemaphoreType.DMA((across,)),
            pltpu.SemaphoreType.DMA((across,)),
            pltpu.SemaphoreType.DMA((4,)),
            pltpu.SemaphoreType.DMA((4,)),
        ],
        compiler_params=pltpu.CompilerParams(
            collective_id=0, has_side_effects=True, vmem_limit_bytes=VMEM_LIMIT
        ),
    )(*(pltpu.with_memory_space_constraint(x, pltpu.HBM) for x in (populations, pore)))
    return pl.pallas_call(
        finish,
        out_shape=jax.ShapeDtypeStruct((count, planes, height, width), jnp.float32),
        in_specs=[pl.BlockSpec(memory_space=pltpu.VMEM)] * 2,
        out_specs=pl.BlockSpec(memory_space=pl.ANY),
        scratch_shapes=[
            pltpu.VMEM((count, planes, height, width), jnp.float32),
            pltpu.SemaphoreType.DMA((count,)),
        ],
        compiler_params=pltpu.CompilerParams(vmem_limit_bytes=VMEM_LIMIT),
    )(post, mask)


def solution(mesh):
    return jax.shard_map(
        functools.partial(body, mesh.shape["px"], mesh.shape["py"]),
        mesh=mesh,
        in_specs=(P(None, None, ("py", "px"), None), P(None, ("py", "px"), None)),
        out_specs=P(None, None, "py", "px"),
        check_vma=False,
    )
```

profile of v0, /device:TPU:0, one launch (start us, length us, event | category | flops | bytes accessed | tf_op | source)
XLA Modules:
  0.0 14.9 jit_solution(14247225170562077641)
XLA Ops:
  0.0 13.8 %shard_map.28 = (f32[19,2,24,384]{3,2,1,0:T(8,128)S(1)}, f32[2,24,384]{2,1,0:T(8,128)S(1)}) custom-call(f32[19,2,8,512]{3,2,1,0:T(8,128)} %pop_ref.1, s32[2,8,512]{2,1,0:T(8,128)} %pore_ref.1), custom_call_target="tpu_custom_call" | custom-call | tf_op jit(solution)/shard_map/pallas_call | solution.py:393
  13.9 1.1 %shard_map.29 = f32[19,2,16,256]{3,2,1,0:T(8,128)} custom-call(f32[19,2,24,384]{3,2,1,0:T(8,128)S(1)} %get-tuple-element.7.post, f32[2,24,384]{2,1,0:T(8,128)S(1)} %get-tuple-element.8.mask), custom_call_target="tpu_custom_call" | custom-call | tf_op jit(solution)/shard_map/pallas_call | solution.py:421
where the time goes:
time: 15.1 us; the launch traced here: 14.9 us
  Pallas kernels  14.9 us (99%)
    pallas_call x1, Pallas kernels, body(): pl.pallas_call(functools.partial(kernel, across, along), out_shape=(pltpu...  13.8 us
    pallas_call x1, Pallas kernels, body(): pl.pallas_call(finish, out_shape=jax.ShapeDtypeStruct((count, planes, hei...  1.06 us

commit v1 on v0

v1 whole, which is shorter than its diff:
```python
import functools

import jax
import jax.numpy as jnp
from jax import lax
from jax.experimental import pallas as pl
from jax.experimental.pallas import tpu as pltpu
from jax.sharding import PartitionSpec as P

MESH = pl.DeviceIdType.MESH

lattice_velocity = [
    (0, 0, 0),
    (1, 0, 0),
    (-1, 0, 0),
    (0, 1, 0),
    (0, -1, 0),
    (0, 0, 1),
    (0, 0, -1),
    (1, 1, 0),
    (-1, -1, 0),
    (1, -1, 0),
    (-1, 1, 0),
    (1, 0, 1),
    (-1, 0, -1),
    (1, 0, -1),
    (-1, 0, 1),
    (0, 1, 1),
    (0, -1, -1),
    (0, 1, -1),
    (0, -1, 1),
]
lattice_weights = [1.0 / 3.0] + [1.0 / 18.0] * 6 + [1.0 / 36.0] * 12
opposite = [0, 2, 1, 4, 3, 6, 5, 8, 7, 10, 9, 12, 11, 14, 13, 16, 15, 18, 17]
relax_time = 0.8
body_force = 0.005

Q = len(lattice_velocity)
LANES = 128
ROWS = 8
HALO = 2
VMEM_LIMIT = 32 * 1024 * 1024
SOLID = -3.0e38
TINY = 1.0e-30

order = sorted(range(Q), key=lambda slot: lattice_velocity[slot][1])
place_of = [order.index(slot) for slot in range(Q)]
RISE = sum(1 for vector in lattice_velocity if vector[1] < 0)
FALL = Q - sum(1 for vector in lattice_velocity if vector[1] > 0)
REST = place_of[0]


def total(values):
    return functools.reduce(lambda x, y: x + y, values)


def collide_tile(fields, is_open, guard, closed):
    keep = 1.0 - 1.0 / relax_time
    gain = 1.0 / relax_time
    density = jnp.where(is_open, total(fields), 1.0)
    inverse = 1.0 / density
    vel = []
    for column in range(3):
        plus = [fields[s] for s in range(Q) if lattice_velocity[s][column] > 0]
        minus = [fields[s] for s in range(Q) if lattice_velocity[s][column] < 0]
        vel.append((total(plus) - total(minus)) * inverse)
    vel[2] = vel[2] + relax_time * body_force
    speed = vel[0] * vel[0] + vel[1] * vel[1] + vel[2] * vel[2]
    base = 1.0 - 1.5 * speed
    result = [None] * Q
    scaled = {w: density * (gain * w) for w in sorted(set(lattice_weights))}

    def close(value):
        return jnp.where(is_open, value + guard if guard else value, closed)

    result[0] = close(keep * fields[0] + scaled[lattice_weights[0]] * base)
    for slot in range(1, Q, 2):
        other = opposite[slot]
        along = None
        for column in range(3):
            sign = lattice_velocity[slot][column]
            if sign == 0:
                continue
            term = vel[column]
            if along is None:
                along = term if sign > 0 else -term
            else:
                along = along + term if sign > 0 else along - term
        weight = scaled[lattice_weights[slot]]
        triple = 3.0 * along
        even = weight * (base + 0.5 * triple * triple)
        odd = weight * triple
        result[slot] = close(keep * fields[slot] + (even + odd))
        result[other] = close(keep * fields[other] + (even - odd))
    return result


def stream(load, sides, slot, plane, tile, closed):
    tiles, planes = sides
    dx, dy, dz = lattice_velocity[slot]
    source = (plane - dz) % planes
    value = load(slot, source, tile, dy)
    if dx:
        lane = lax.broadcasted_iota(jnp.int32, value.shape, 1)
        beside = load(slot, source, (tile - dx) % tiles, dy)
        value = jnp.where(lane == (LANES - 1 if dx > 0 else 0), beside, value)
        value = pltpu.roll(value, dx % LANES, 1)
    if slot:
        value = jnp.where(value != closed, value, load(opposite[slot], plane, tile, 0))
    return value


def kernel(
    across, along, pop_ref, pore_ref, post2,
    raw, voxels, box, post, sides, ring, packs, edges, ring_edges,
    load_sem, n_send, n_recv, h_send, h_recv,
):
    _, planes, strips, rows, _ = box.shape
    wt = strips // across
    height = across * rows
    groups = edges.shape[0]
    per_group = LANES // 4
    slabs = Q * planes
    me = lax.axis_index("px")
    here = lax.axis_index("py")
    up = lax.rem(here + along - 1, along)
    down = lax.rem(here + 1, along)

    load_pore = pltpu.make_async_copy(pore_ref, voxels, load_sem.at[0])
    load_pore.start()

    def load_tile(step, k):
        tile = lax.rem(me + step, across) * wt + k
        cols = pl.ds(pl.multiple_of(tile * LANES, LANES), LANES)
        return pltpu.make_async_copy(
            pop_ref.at[:, :, :, cols], raw.at[:, :, tile], load_sem.at[1 + (step - 1) * wt + k]
        )

    for step in range(1, across + 1):
        for k in range(wt):
            load_tile(step, k).start()

    barrier = pltpu.get_barrier_semaphore()
    for step in range(1, across):
        pl.semaphore_signal(barrier, inc=1, device_id=(lax.rem(me + step, across), here), device_id_type=MESH)
    for to in (up, down):
        pl.semaphore_signal(barrier, inc=1, device_id=(me, to), device_id_type=MESH)
    load_pore.wait()

    def collide_strip(tile, own):
        cols = pl.ds(pl.multiple_of(tile * LANES, LANES), LANES)
        for plane in range(planes):
            fields = [raw[slot, plane, tile] for slot in range(Q)]
            is_open = voxels[plane, :, cols] > 0
            result = collide_tile(fields, is_open, TINY, 0.0)
            for slot in range(Q):
                box[place_of[slot], plane, tile] = result[slot]
                if own is not None:
                    at = pl.ds(pl.multiple_of(me * rows, ROWS), rows)
                    post[place_of[slot], plane, own, at, :] = result[slot]

    def outer(source):
        return (rows - HALO, rows) if source == across - 1 else (0, HALO)

    def inner(source):
        return (0, HALO) if source == across - 1 else (rows - HALO, rows)

    def rest(source):
        return (0, rows - HALO) if source == across - 1 else (HALO, rows)

    def middle(source):
        return (HALO, rows - HALO)

    def send(source, target, n):
        if n == 1:
            src, dst = packs.at[target], edges.at[:, source * rows : (source + 1) * rows, :]
        else:
            low, high = (outer, None, rest, inner, middle)[n](source)
            first, last = ((0, wt), None, (0, wt - 1), (wt - 1, wt), (wt - 1, wt))[n]
            src = box.at[:, :, target * wt + first : target * wt + last, low:high, :]
            start = source * rows
            dst = post.at[:, :, first:last, start + low : start + high, :]
        return pltpu.make_async_remote_copy(
            src_ref=src,
            dst_ref=dst,
            send_sem=n_send.at[target, n],
            recv_sem=n_recv.at[source, n],
            device_id=(target, here),
            device_id_type=MESH,
        )

    pieces = [0, 1, 2, 3, 4] if wt > 1 else [0, 1, 3, 4]

    def relay(way):
        if way == 0:
            near, beyond, part, to = 0, 1, (0, RISE), up
            near_to, beyond_to, low, low_to = ROWS - 2, ROWS - 1, 0, ROWS - HALO
        else:
            near, beyond, part, to = height - 1, height - 2, (FALL, Q), down
            near_to, beyond_to, low, low_to = 1, 0, height - HALO, 0
        some = slice(*part)
        refs = [
            (post.at[:, :, :, near : near + 1, :],
             ring.at[:, :, 0:wt, near_to : near_to + 1, :]),
            (post.at[some, :, :, beyond : beyond + 1, :],
             ring.at[some, :, 0:wt, beyond_to : beyond_to + 1, :]),
            (edges.at[:, low : low + HALO, :], ring_edges.at[:, low_to : low_to + HALO, :]),
        ]
        return [
            pltpu.make_async_remote_copy(
                src_ref=src,
                dst_ref=dst,
                send_sem=h_send.at[way, n],
                recv_sem=h_recv.at[way, n],
                device_id=(me, to),
                device_id_type=MESH,
            )
            for n, (src, dst) in enumerate(refs)
        ]

    def peers(mine):
        return [(mine + step) % across for step in range(1, across)]

    def on_each(action):
        for mine in range(across):
            pl.when(me == mine)(functools.partial(action, mine))

    def begin(wanted):
        def action(mine):
            for n in pieces:
                if n in wanted:
                    for target in peers(mine):
                        send(mine, target, n).start()

        on_each(action)

    for step in range(1, across):
        for k in range(wt):
            load_tile(step, k).wait()
            collide_strip(lax.rem(me + step, across) * wt + k, None)
        if step == 1:
            pl.semaphore_wait(barrier, across - 1 + 2)
    begin((0,))
    for k in range(wt):
        load_tile(across, k).wait()
        collide_strip(me * wt + k, k)

    lane = lax.broadcasted_iota(jnp.int32, (rows, LANES), 1)
    for step in range(1, across + 1):
        target = lax.rem(me + step, across)
        first = lax.rem((target + 1) * wt, strips)
        last = lax.rem(target * wt + strips - 1, strips)
        own_at = pl.ds(pl.multiple_of(me * rows, ROWS), rows)
        for group in range(groups):
            packed = jnp.zeros((rows, LANES), jnp.float32)
            for place in range(per_group):
                slab = group * per_group + place
                if slab >= slabs:
                    break
                field, plane = slab // planes, slab % planes
                edge = jnp.where(lane < LANES // 2, box[field, plane, first], box[field, plane, last])
                if step == across:
                    sides[field, plane, own_at, :] = edge
                if place == 0:
                    packed = edge
                else:
                    moved = pltpu.roll(edge, 4 * place, 1)
                    packed = jnp.where((lane >= 4 * place - 2) & (lane < 4 * place + 2), moved, packed)
            if step == across:
                edges[group, own_at, :] = packed
            else:
                packs[target, group] = packed
        if step == across - 1:
            begin((1, 2, 3, 4))

    ends = ((0, 0), (across - 1, 1))

    def relay_own(mine):
        for source, way in ends:
            if source == mine:
                for copy in relay(way):
                    copy.start()

    on_each(relay_own)

    def unpack(packs_of, at, store):
        for slab in range(slabs):
            group, place = slab // per_group, slab % per_group
            packed = packs_of[group, at, :]
            moved = pltpu.roll(packed, LANES - 4 * place, 1) if place else packed
            store(slab // planes, slab % planes, moved)

    def relay_rest(mine):
        for source in peers(mine):
            send(source, mine, 0).wait_recv()
            send(source, mine, 1).wait_recv()
            for end, way in ends:
                if source == end:
                    for copy in relay(way):
                        copy.start()

    on_each(relay_rest)

    def settle(wanted):
        def action(mine):
            for source in peers(mine):
                for n in pieces:
                    if n in wanted:
                        send(source, mine, n).wait_recv()

        on_each(action)

    def advance(load, store):
        for plane in range(planes):
            for tile in range(wt + 1):
                is_open = load(0, plane, tile, 0) != 0.0
                fields = [stream(load, (wt + 1, planes), slot, plane, tile, 0.0) for slot in range(Q)]
                result = collide_tile(fields, is_open, None, SOLID)
                for slot in range(Q):
                    store(slot, plane, tile, result[slot])

    def window(source):
        start = jnp.minimum(rows * source + 1, height - 1 - ROWS)

        def load(slot, plane, tile, dy):
            at = pl.ds(start - dy, ROWS)
            if tile == wt:
                return sides[place_of[slot], plane, at, :]
            return post[place_of[slot], plane, tile, at, :]

        def store(slot, plane, tile, value):
            post2[place_of[slot], plane, tile, pl.ds(ROWS + start, ROWS), :] = value

        advance(load, store)

    row = lax.broadcasted_iota(jnp.int32, (ROWS, LANES), 0)
    half = ROWS // 2

    def fill():
        for slot in range(Q):
            for plane in range(planes):
                for tile in range(wt):
                    ring[slot, plane, tile, HALO:half, :] = post[slot, plane, tile, 0:HALO, :]
                    ring[slot, plane, tile, half : half + HALO, :] = post[
                        slot, plane, tile, height - HALO : height, :
                    ]
        for group in range(groups):
            ring_edges[group, HALO:half, :] = edges[group, 0:HALO, :]
            ring_edges[group, half : half + HALO, :] = edges[group, height - HALO : height, :]

    def rim():
        top, low = ROWS - HALO, height + HALO

        def load(slot, plane, tile, dy):
            value = ring[place_of[slot], plane, tile]
            return pltpu.roll(value, dy % ROWS, 0) if dy else value

        def store(slot, plane, tile, value):
            place = place_of[slot]
            pltpu.store(
                post2.at[place, plane, tile, top : top + ROWS, :], value,
                mask=(row >= 1) & (row < 3),
            )
            pltpu.store(
                post2.at[place, plane, tile, low : low + ROWS, :], value,
                mask=(row >= half + 1) & (row < half + 3),
            )

        advance(load, store)

    def unpack_from(step, carry):
        at = pl.ds(pl.multiple_of(lax.rem(me + step, across) * rows, ROWS), rows)

        def store(slot, plane, value):
            sides[slot, plane, at, :] = value

        unpack(edges, at, store)
        return carry

    def unpack_ring():
        def store(slot, plane, value):
            ring[slot, plane, wt] = value

        unpack(ring_edges, pl.ds(0, ROWS), store)

    lax.fori_loop(1, across, unpack_from, 0)
    fill()
    settle((2, 3))
    window(me)
    for way in range(2):
        for copy in relay(way):
            copy.wait_recv()
    unpack_ring()
    rim()
    settle((4,))

    def window_from(step, carry):
        window(lax.rem(me + step, across))
        return carry

    lax.fori_loop(1, across, window_from, 0)

    def sent(mine):
        for target in peers(mine):
            for n in pieces:
                send(mine, target, n).wait_send()
        for way in range(2):
            for copy in relay(way):
                copy.wait_send()

    on_each(sent)


def finish(post, out_ref, flow, sems):
    _, planes, height, width = flow.shape
    wt = width // LANES

    def load(slot, plane, tile, dy):
        return post[place_of[slot], plane, tile, at - dy : at - dy + ROWS, :]

    copies = []
    for slot in range(Q):
        for plane in range(planes):
            for tile in range(wt):
                for start in range(0, height, ROWS):
                    at = ROWS + start
                    is_open = load(0, plane, tile, 0) != SOLID
                    value = stream(load, (wt + 1, planes), slot, plane, tile, SOLID)
                    flow[slot, plane, start : start + ROWS, tile * LANES : (tile + 1) * LANES] = jnp.where(
                        is_open, value, 0.0
                    )
        copies.append(pltpu.make_async_copy(flow.at[slot], out_ref.at[slot], sems.at[slot]))
        if slot:
            copies[slot - 1].start()
    copies[-1].start()
    for copy in copies:
        copy.wait()


def body(across, along, populations, pore):
    count, planes, rows, columns = populations.shape
    height = across * rows
    width = columns // across
    strips = columns // LANES
    wt = strips // across
    groups = -(-count * planes * 4 // LANES)
    tall = height + 2 * ROWS
    post2 = pl.pallas_call(
        functools.partial(kernel, across, along),
        out_shape=pltpu.VMEM((count, planes, wt + 1, tall, LANES), jnp.float32),
        in_specs=[pl.BlockSpec(memory_space=pltpu.HBM)] * 2,
        out_specs=pl.BlockSpec(memory_space=pltpu.VMEM),
        scratch_shapes=[
            pltpu.VMEM((count, planes, strips, rows, LANES), jnp.float32),
            pltpu.VMEM((planes, rows, columns), jnp.int32),
            pltpu.VMEM((count, planes, strips, rows, LANES), jnp.float32),
            pltpu.VMEM((count, planes, wt, height, LANES), jnp.float32),
            pltpu.VMEM((count, planes, height, LANES), jnp.float32),
            pltpu.VMEM((count, planes, wt + 1, ROWS, LANES), jnp.float32),
            pltpu.VMEM((across, groups, rows, LANES), jnp.float32),
            pltpu.VMEM((groups, height, LANES), jnp.float32),
            pltpu.VMEM((groups, ROWS, LANES), jnp.float32),
            pltpu.SemaphoreType.DMA((1 + strips,)),
            pltpu.SemaphoreType.DMA((across, 5)),
            pltpu.SemaphoreType.DMA((across, 5)),
            pltpu.SemaphoreType.DMA((2, 3)),
            pltpu.SemaphoreType.DMA((2, 3)),
        ],
        compiler_params=pltpu.CompilerParams(
            collective_id=0, has_side_effects=True, vmem_limit_bytes=VMEM_LIMIT
        ),
    )(*(pltpu.with_memory_space_constraint(x, pltpu.HBM) for x in (populations, pore)))
    return pl.pallas_call(
        finish,
        out_shape=jax.ShapeDtypeStruct((count, planes, height, width), jnp.float32),
        in_specs=[pl.BlockSpec(memory_space=pltpu.VMEM)],
        out_specs=pl.BlockSpec(memory_space=pl.ANY),
        scratch_shapes=[
            pltpu.VMEM((count, planes, height, width), jnp.float32),
            pltpu.SemaphoreType.DMA((count,)),
        ],
        compiler_params=pltpu.CompilerParams(vmem_limit_bytes=VMEM_LIMIT),
    )(post2)


def solution(mesh):
    return jax.shard_map(
        functools.partial(body, mesh.shape["px"], mesh.shape["py"]),
        mesh=mesh,
        in_specs=(P(None, None, ("py", "px"), None), P(None, ("py", "px"), None)),
        out_specs=P(None, None, "py", "px"),
        check_vma=False,
    )
```

time: 15.1 us -> 14.1 us (0.934)
  Pallas kernels: 14.9 us -> 14 us
    pallas_call x1, Pallas kernels: 13.8 us -> 12.9 us  [body(): pl.pallas_call(functools.partial(kernel, across, along), out_shape=pltpu....]
where the time goes in v1:
time: 14.1 us; the launch traced here: 14 us
  Pallas kernels  14 us (99%)
    pallas_call x1, Pallas kernels, body(): pl.pallas_call(functools.partial(kernel, across, along), out_shape=pltpu....  12.9 us
    pallas_call x1, Pallas kernels, body(): pl.pallas_call(finish, out_shape=jax.ShapeDtypeStruct((count, planes, hei...  1.06 us

profile of v1, /device:TPU:0, one launch (start us, length us, event | category | flops | bytes accessed | tf_op | source)
XLA Modules:
  0.0 14.0 jit_solution(3840394030932650661)
XLA Ops:
  0.0 12.9 %shard_map.28.post = f32[19,2,3,32,128]{4,3,2,1,0:T(8,128)S(1)} custom-call(f32[19,2,8,512]{3,2,1,0:T(8,128)} %pop_ref.1, s32[2,8,512]{2,1,0:T(8,128)} %pore_ref.1), custom_call_target="tpu_custom_call" | custom-call | tf_op jit(solution)/shard_map/pallas_call | solution.py:448
  12.9 1.1 %shard_map.29 = f32[19,2,16,256]{3,2,1,0:T(8,128)} custom-call(f32[19,2,3,32,128]{4,3,2,1,0:T(8,128)S(1)} %shard_map.28.post), custom_call_target="tpu_custom_call" | custom-call | tf_op jit(solution)/shard_map/pallas_call | solution.py:473

commit v2 on v1

--- a/solution.py
+++ b/solution.py
@@ -113,7 +113,7 @@
 def kernel(
     across, along, pop_ref, pore_ref, post2,
     raw, voxels, box, post, sides, ring, packs, edges, ring_edges,
-    load_sem, n_send, n_recv, h_send, h_recv,
+    load_sem, n_send, n_recv, h_send, h_recv, w_send, go,
 ):
     _, planes, strips, rows, _ = box.shape
     wt = strips // across
@@ -125,6 +125,10 @@
     here = lax.axis_index("py")
     up = lax.rem(here + along - 1, along)
     down = lax.rem(here + 1, along)
+    first_row = here == 0
+    last_row = here == along - 1
+    odd = lax.rem(here, 2) == 1
+    eager = odd & (here != along - 1)
 
     load_pore = pltpu.make_async_copy(pore_ref, voxels, load_sem.at[0])
     load_pore.start()
@@ -141,10 +145,57 @@
             load_tile(step, k).start()
 
     barrier = pltpu.get_barrier_semaphore()
+
+    def greet(x, y):
+        pl.semaphore_signal(barrier, inc=1, device_id=(x, y), device_id_type=MESH)
+
     for step in range(1, across):
-        pl.semaphore_signal(barrier, inc=1, device_id=(lax.rem(me + step, across), here), device_id_type=MESH)
-    for to in (up, down):
-        pl.semaphore_signal(barrier, inc=1, device_id=(me, to), device_id_type=MESH)
+        greet(lax.rem(me + step, across), here)
+
+    @pl.when(here == along - 2)
+    def _():
+        greet(me, down)
+
+    @pl.when(last_row)
+    def _():
+        greet(me, up)
+
+    @pl.when(eager)
+    def _():
+        pl.semaphore_wait(barrier, across - 1)
+        greet(me, up)
+        greet(me, down)
+
+    def enter():
+        @pl.when(first_row)
+        def _():
+            pl.semaphore_wait(barrier, across - 1 + 1)
+            greet(me, down)
+            greet(me, along - 1)
+
+            @pl.when(me != across - 1)
+            def _():
+                greet(across - 1, along - 1)
+
+        @pl.when(last_row & (me != across - 1))
+        def _():
+            pl.semaphore_wait(barrier, across - 1 + 2)
+            greet(me, 0)
+
+        @pl.when(last_row & (me == across - 1))
+        def _():
+            pl.semaphore_wait(barrier, across - 1 + 2 + across - 1)
+            greet(me, 0)
+
+        @pl.when(jnp.logical_not(odd) & (here != 0))
+        def _():
+            pl.semaphore_wait(barrier, across - 1 + 2)
+            greet(me, up)
+
+            @pl.when(here != along - 2)
+            def _():
+                greet(me, down)
+
     load_pore.wait()
 
     def collide_strip(tile, own):
@@ -239,7 +290,7 @@
             load_tile(step, k).wait()
             collide_strip(lax.rem(me + step, across) * wt + k, None)
         if step == 1:
-            pl.semaphore_wait(barrier, across - 1 + 2)
+            enter()
     begin((0,))
     for k in range(wt):
         load_tile(across, k).wait()
@@ -266,22 +317,64 @@
                 else:
                     moved = pltpu.roll(edge, 4 * place, 1)
                     packed = jnp.where((lane >= 4 * place - 2) & (lane < 4 * place + 2), moved, packed)
+            packs[target, group] = packed
             if step == across:
                 edges[group, own_at, :] = packed
-            else:
-                packs[target, group] = packed
         if step == across - 1:
-            begin((1, 2, 3, 4))
+            begin((1,))
+
+            @pl.when(jnp.logical_not(odd))
+            def _():
+                begin((2, 3, 4))
 
     ends = ((0, 0), (across - 1, 1))
 
-    def relay_own(mine):
-        for source, way in ends:
-            if source == mine:
-                for copy in relay(way):
-                    copy.start()
-
-    on_each(relay_own)
+    def direct(target):
+        cols = slice(target * wt, (target + 1) * wt)
+        refs = [
+            (box.at[:, :, cols, rows - 1 : rows, :], ring.at[:, :, 0:wt, 1:2, :]),
+            (box.at[FALL:Q, :, cols, rows - HALO : rows - 1, :], ring.at[FALL:Q, :, 0:wt, 0:1, :]),
+            (packs.at[target, :, rows - HALO : rows, :], ring_edges.at[:, 0:HALO, :]),
+        ]
+        return [
+            pltpu.make_async_remote_copy(
+                src_ref=src,
+                dst_ref=dst,
+                send_sem=w_send.at[target, n],
+                recv_sem=h_recv.at[1, n],
+                device_id=(target, 0),
+                device_id_type=MESH,
+            )
+            for n, (src, dst) in enumerate(refs)
+        ]
+
+    last_strip = last_row & (me == across - 1)
+
+    @pl.when(last_strip)
+    def _():
+        for target in range(across):
+            for copy in direct(target):
+                copy.start()
+
+    lead = 2 if wt > 1 else 3
+
+    @pl.when(odd)
+    def _():
+        pl.semaphore_wait(go, 1)
+        begin((2, 3, 4))
+
+    def lead_sent(mine):
+        for target in peers(mine):
+            send(mine, target, lead).wait_send()
+
+    @pl.when(jnp.logical_not(odd))
+    def _():
+        on_each(lead_sent)
+        pl.semaphore_signal(go, inc=1, device_id=(me, down), device_id_type=MESH)
+
+    @pl.when(eager)
+    def _():
+        pl.semaphore_wait(barrier, 2)
 
     def unpack(packs_of, at, store):
         for slab in range(slabs):
@@ -290,16 +383,38 @@
             moved = pltpu.roll(packed, LANES - 4 * place, 1) if place else packed
             store(slab // planes, slab % planes, moved)
 
-    def relay_rest(mine):
-        for source in peers(mine):
+    def pass_on(mine, source, way):
+        if source != mine:
             send(source, mine, 0).wait_recv()
             send(source, mine, 1).wait_recv()
-            for end, way in ends:
-                if source == end:
-                    for copy in relay(way):
-                        copy.start()
-
-    on_each(relay_rest)
+
+        def start():
+            for copy in relay(way):
+                copy.start()
+
+        if way:
+            pl.when(jnp.logical_not(last_row))(start)
+        else:
+            start()
+
+    def relays(mine):
+        @pl.when(first_row)
+        def _():
+            pass_on(mine, across - 1, 1)
+            pl.semaphore_wait(barrier, 1)
+            pass_on(mine, 0, 0)
+
+        @pl.when(jnp.logical_not(first_row))
+        def _():
+            for source, way in sorted(ends, key=lambda end: end[0] != mine):
+                pass_on(mine, source, way)
+
+        for source in peers(mine):
+            if source not in (0, across - 1):
+                send(source, mine, 0).wait_recv()
+                send(source, mine, 1).wait_recv()
+
+    on_each(relays)
 
     def settle(wanted):
         def action(mine):
@@ -403,12 +518,25 @@
     def sent(mine):
         for target in peers(mine):
             for n in pieces:
-                send(mine, target, n).wait_send()
-        for way in range(2):
-            for copy in relay(way):
+                if n == lead:
+                    pl.when(odd)(send(mine, target, n).wait_send)
+                else:
+                    send(mine, target, n).wait_send()
+
+    on_each(sent)
+    for copy in relay(0):
+        copy.wait_send()
+
+    @pl.when(jnp.logical_not(last_row))
+    def _():
+        for copy in relay(1):
+            copy.wait_send()
+
+    @pl.when(last_strip)
+    def _():
+        for target in range(across):
+            for copy in direct(target):
                 copy.wait_send()
-
-    on_each(sent)
 
 
 def finish(post, out_ref, flow, sems):
@@ -465,6 +593,8 @@
             pltpu.SemaphoreType.DMA((across, 5)),
             pltpu.SemaphoreType.DMA((2, 3)),
             pltpu.SemaphoreType.DMA((2, 3)),
+            pltpu.SemaphoreType.DMA((across, 3)),
+            pltpu.SemaphoreType.REGULAR,
         ],
         compiler_params=pltpu.CompilerParams(
             collective_id=0, has_side_effects=True, vmem_limit_bytes=VMEM_LIMIT

time: 14.1 us -> 12.9 us (0.915)
  the two profiles are of different devices: /device:TPU:0 before, /device:TPU:1 now
where the time goes in v2:
time: 12.9 us; the launch traced here: 12.7 us
  Pallas kernels  12.7 us (98%)
    pallas_call x1, Pallas kernels, body(): pl.pallas_call(functools.partial(kernel, across, along), out_shape=pltpu....  11.6 us
    pallas_call x1, Pallas kernels, body(): pl.pallas_call(finish, out_shape=jax.ShapeDtypeStruct((count, planes, hei...  1.06 us

profile of v2, /device:TPU:1, one launch (start us, length us, event | category | flops | bytes accessed | tf_op | source)
XLA Modules:
  0.0 12.7 jit_solution(1055781650721223293)
XLA Ops:
  0.0 11.6 %shard_map.28.post = f32[19,2,3,32,128]{4,3,2,1,0:T(8,128)S(1)} custom-call(f32[19,2,8,512]{3,2,1,0:T(8,128)} %pop_ref.1, s32[2,8,512]{2,1,0:T(8,128)} %pore_ref.1), custom_call_target="tpu_custom_call" | custom-call | tf_op jit(solution)/shard_map/pallas_call | solution.py:576
  11.6 1.1 %shard_map.29 = f32[19,2,16,256]{3,2,1,0:T(8,128)} custom-call(f32[19,2,3,32,128]{4,3,2,1,0:T(8,128)S(1)} %shard_map.28.post), custom_call_target="tpu_custom_call" | custom-call | tf_op jit(solution)/shard_map/pallas_call | solution.py:603

commit v3 on v2

--- a/solution.py
+++ b/solution.py
@@ -47,7 +47,7 @@
 place_of = [order.index(slot) for slot in range(Q)]
 RISE = sum(1 for vector in lattice_velocity if vector[1] < 0)
 FALL = Q - sum(1 for vector in lattice_velocity if vector[1] > 0)
-REST = place_of[0]
+PAIRS = [(s, opposite[s]) for s in range(Q) if lattice_velocity[s][0] > 0]
 
 
 def total(values):
@@ -95,14 +95,14 @@
     return result
 
 
-def stream(load, sides, slot, plane, tile, closed):
+def stream(load, sides, slot, plane, tile, closed, seam=None):
     tiles, planes = sides
     dx, dy, dz = lattice_velocity[slot]
     source = (plane - dz) % planes
     value = load(slot, source, tile, dy)
     if dx:
         lane = lax.broadcasted_iota(jnp.int32, value.shape, 1)
-        beside = load(slot, source, (tile - dx) % tiles, dy)
+        beside = (seam or load)(slot, source, (tile - dx) % tiles, dy)
         value = jnp.where(lane == (LANES - 1 if dx > 0 else 0), beside, value)
         value = pltpu.roll(value, dx % LANES, 1)
     if slot:
@@ -112,8 +112,8 @@
 
 def kernel(
     across, along, pop_ref, pore_ref, post2,
-    raw, voxels, box, post, sides, ring, packs, edges, ring_edges,
-    load_sem, n_send, n_recv, h_send, h_recv, w_send, go,
+    raw, voxels, box, post, sides, seams, ring, packs, edges, ring_edges,
+    load_sem, n_send, n_recv, h_send, h_recv, w_send, go, ready,
 ):
     _, planes, strips, rows, _ = box.shape
     wt = strips // across
@@ -128,87 +128,81 @@
     first_row = here == 0
     last_row = here == along - 1
     odd = lax.rem(here, 2) == 1
-    eager = odd & (here != along - 1)
+    last_strip = last_row & (me == across - 1)
 
     load_pore = pltpu.make_async_copy(pore_ref, voxels, load_sem.at[0])
     load_pore.start()
 
-    def load_tile(step, k):
+    def load_tile(step, k, plane):
         tile = lax.rem(me + step, across) * wt + k
         cols = pl.ds(pl.multiple_of(tile * LANES, LANES), LANES)
         return pltpu.make_async_copy(
-            pop_ref.at[:, :, :, cols], raw.at[:, :, tile], load_sem.at[1 + (step - 1) * wt + k]
+            pop_ref.at[:, plane, :, cols],
+            raw.at[:, plane, tile],
+            load_sem.at[1 + ((step - 1) * wt + k) * planes + plane],
         )
 
+    halves = [(k, plane) for k in range(wt) for plane in range(planes)]
     for step in range(1, across + 1):
-        for k in range(wt):
-            load_tile(step, k).start()
+        for k, plane in halves:
+            load_tile(step, k, plane).start()
 
     barrier = pltpu.get_barrier_semaphore()
 
     def greet(x, y):
         pl.semaphore_signal(barrier, inc=1, device_id=(x, y), device_id_type=MESH)
 
+    def answer(y):
+        pl.semaphore_signal(ready, inc=1, device_id=(me, y), device_id_type=MESH)
+
     for step in range(1, across):
         greet(lax.rem(me + step, across), here)
 
-    @pl.when(here == along - 2)
-    def _():
-        greet(me, down)
-
-    @pl.when(last_row)
+    @pl.when(odd)
     def _():
         greet(me, up)
 
-    @pl.when(eager)
+        @pl.when(jnp.logical_not(last_row))
+        def _():
+            greet(me, down)
+
+    @pl.when(first_row)
     def _():
-        pl.semaphore_wait(barrier, across - 1)
-        greet(me, up)
-        greet(me, down)
+        greet(me, along - 1)
+
+        @pl.when(me != across - 1)
+        def _():
+            greet(across - 1, along - 1)
 
     def enter():
-        @pl.when(first_row)
+        greeted = jnp.where(odd, 0, 2) - jnp.where(first_row, 1, 0)
+        greeted = greeted + jnp.where(last_row, jnp.where(me == across - 1, across, 1), 0)
+        pl.semaphore_wait(barrier, across - 1 + greeted)
+
+        @pl.when(jnp.logical_not(odd))
         def _():
-            pl.semaphore_wait(barrier, across - 1 + 1)
-            greet(me, down)
-            greet(me, along - 1)
-
-            @pl.when(me != across - 1)
+            answer(down)
+
+            @pl.when(here != 0)
             def _():
-                greet(across - 1, along - 1)
-
-        @pl.when(last_row & (me != across - 1))
+                answer(up)
+
+        @pl.when(last_row)
         def _():
-            pl.semaphore_wait(barrier, across - 1 + 2)
-            greet(me, 0)
-
-        @pl.when(last_row & (me == across - 1))
-        def _():
-            pl.semaphore_wait(barrier, across - 1 + 2 + across - 1)
-            greet(me, 0)
-
-        @pl.when(jnp.logical_not(odd) & (here != 0))
-        def _():
-            pl.semaphore_wait(barrier, across - 1 + 2)
-            greet(me, up)
-
-            @pl.when(here != along - 2)
-            def _():
-                greet(me, down)
+            answer(0)
 
     load_pore.wait()
 
-    def collide_strip(tile, own):
+    def collide_strip(tile, plane, own):
         cols = pl.ds(pl.multiple_of(tile * LANES, LANES), LANES)
-        for plane in range(planes):
-            fields = [raw[slot, plane, tile] for slot in range(Q)]
-            is_open = voxels[plane, :, cols] > 0
-            result = collide_tile(fields, is_open, TINY, 0.0)
-            for slot in range(Q):
-                box[place_of[slot], plane, tile] = result[slot]
-                if own is not None:
-                    at = pl.ds(pl.multiple_of(me * rows, ROWS), rows)
-                    post[place_of[slot], plane, own, at, :] = result[slot]
+        fields = [raw[slot, plane, tile] for slot in range(Q)]
+        is_open = voxels[plane, :, cols] > 0
+        result = collide_tile(fields, is_open, TINY, 0.0)
+        for slot in range(Q):
+            box[place_of[slot], plane, tile] = result[slot]
+            if own is not None:
+                at = pl.ds(pl.multiple_of(me * rows, ROWS), rows)
+                post[place_of[slot], plane, own, at, :] = result[slot]
 
     def outer(source):
         return (rows - HALO, rows) if source == across - 1 else (0, HALO)
@@ -222,7 +216,18 @@
     def middle(source):
         return (HALO, rows - HALO)
 
-    def send(source, target, n):
+    def send(source, target, n, part=None):
+        if part:
+            k, plane = part
+            low, high = outer(source)
+            return pltpu.make_async_remote_copy(
+                src_ref=box.at[:, plane, target * wt + k, low:high, :],
+                dst_ref=post.at[:, plane, k, source * rows + low : source * rows + high, :],
+                send_sem=n_send.at[target, n],
+                recv_sem=n_recv.at[source, n],
+                device_id=(target, here),
+                device_id_type=MESH,
+            )
         if n == 1:
             src, dst = packs.at[target], edges.at[:, source * rows : (source + 1) * rows, :]
         else:
@@ -285,51 +290,7 @@
 
         on_each(action)
 
-    for step in range(1, across):
-        for k in range(wt):
-            load_tile(step, k).wait()
-            collide_strip(lax.rem(me + step, across) * wt + k, None)
-        if step == 1:
-            enter()
-    begin((0,))
-    for k in range(wt):
-        load_tile(across, k).wait()
-        collide_strip(me * wt + k, k)
-
-    lane = lax.broadcasted_iota(jnp.int32, (rows, LANES), 1)
-    for step in range(1, across + 1):
-        target = lax.rem(me + step, across)
-        first = lax.rem((target + 1) * wt, strips)
-        last = lax.rem(target * wt + strips - 1, strips)
-        own_at = pl.ds(pl.multiple_of(me * rows, ROWS), rows)
-        for group in range(groups):
-            packed = jnp.zeros((rows, LANES), jnp.float32)
-            for place in range(per_group):
-                slab = group * per_group + place
-                if slab >= slabs:
-                    break
-                field, plane = slab // planes, slab % planes
-                edge = jnp.where(lane < LANES // 2, box[field, plane, first], box[field, plane, last])
-                if step == across:
-                    sides[field, plane, own_at, :] = edge
-                if place == 0:
-                    packed = edge
-                else:
-                    moved = pltpu.roll(edge, 4 * place, 1)
-                    packed = jnp.where((lane >= 4 * place - 2) & (lane < 4 * place + 2), moved, packed)
-            packs[target, group] = packed
-            if step == across:
-                edges[group, own_at, :] = packed
-        if step == across - 1:
-            begin((1,))
-
-            @pl.when(jnp.logical_not(odd))
-            def _():
-                begin((2, 3, 4))
-
-    ends = ((0, 0), (across - 1, 1))
-
-    def direct(target):
+    def direct(target, which=range(3)):
         cols = slice(target * wt, (target + 1) * wt)
         refs = [
             (box.at[:, :, cols, rows - 1 : rows, :], ring.at[:, :, 0:wt, 1:2, :]),
@@ -346,15 +307,74 @@
                 device_id_type=MESH,
             )
             for n, (src, dst) in enumerate(refs)
+            if n in which
         ]
 
-    last_strip = last_row & (me == across - 1)
-
-    @pl.when(last_strip)
-    def _():
-        for target in range(across):
-            for copy in direct(target):
-                copy.start()
+    def send_direct(targets, which):
+        @pl.when(last_strip)
+        def _():
+            for target in targets:
+                for copy in direct(target, which):
+                    copy.start()
+
+
+    for step in range(1, across):
+        for k, plane in halves:
+            load_tile(step, k, plane).wait()
+            collide_strip(lax.rem(me + step, across) * wt + k, plane, None)
+            if step == 1 and (k, plane) == (0, 0):
+                enter()
+
+            def begin_outer(mine):
+                send(mine, (mine + step) % across, 0, (k, plane)).start()
+
+            on_each(begin_outer)
+    send_direct(range(across - 1), (0, 1))
+    for k, plane in halves:
+        load_tile(across, k, plane).wait()
+        collide_strip(me * wt + k, plane, k)
+    send_direct((across - 1,), (0, 1))
+
+    lane = lax.broadcasted_iota(jnp.int32, (rows, LANES), 1)
+    for step in range(1, across + 1):
+        target = lax.rem(me + step, across)
+        first = lax.rem((target + 1) * wt, strips)
+        last = lax.rem(target * wt + strips - 1, strips)
+        own_at = pl.ds(pl.multiple_of(me * rows, ROWS), rows)
+        for group in range(groups):
+            packed = jnp.zeros((rows, LANES), jnp.float32)
+            for place in range(per_group):
+                slab = group * per_group + place
+                if slab >= slabs + len(PAIRS) * planes:
+                    break
+                field, plane = slab // planes, slab % planes
+                if slab < slabs:
+                    edge = jnp.where(lane < LANES // 2, box[field, plane, first], box[field, plane, last])
+                    if step == across:
+                        sides[field, plane, own_at, :] = edge
+                else:
+                    right, left = (place_of[slot] for slot in PAIRS[field - Q])
+                    tile = target * wt + wt - 1
+                    edge = jnp.where(lane < LANES // 2, box[left, plane, tile], box[right, plane, tile])
+                    if step == across:
+                        seams[field - Q, plane, own_at, :] = edge
+                if place == 0:
+                    packed = edge
+                else:
+                    moved = pltpu.roll(edge, 4 * place, 1)
+                    packed = jnp.where((lane >= 4 * place - 2) & (lane < 4 * place + 2), moved, packed)
+            packs[target, group] = packed
+            if step == across:
+                edges[group, own_at, :] = packed
+        if step == across - 1:
+            begin((1,))
+
+            @pl.when(jnp.logical_not(odd))
+            def _():
+                begin((2, 3, 4))
+
+    send_direct(range(across), (2,))
+    ends = ((0, 0), (across - 1, 1))
 
     lead = 2 if wt > 1 else 3
 
@@ -372,12 +392,12 @@
         on_each(lead_sent)
         pl.semaphore_signal(go, inc=1, device_id=(me, down), device_id_type=MESH)
 
-    @pl.when(eager)
+    @pl.when(odd)
     def _():
-        pl.semaphore_wait(barrier, 2)
+        pl.semaphore_wait(ready, jnp.where(last_row, 1, 2))
 
     def unpack(packs_of, at, store):
-        for slab in range(slabs):
+        for slab in range(slabs + len(PAIRS) * planes):
             group, place = slab // per_group, slab % per_group
             packed = packs_of[group, at, :]
             moved = pltpu.roll(packed, LANES - 4 * place, 1) if place else packed
@@ -401,7 +421,7 @@
         @pl.when(first_row)
         def _():
             pass_on(mine, across - 1, 1)
-            pl.semaphore_wait(barrier, 1)
+            pl.semaphore_wait(ready, 1)
             pass_on(mine, 0, 0)
 
         @pl.when(jnp.logical_not(first_row))
@@ -425,16 +445,19 @@
 
         on_each(action)
 
-    def advance(load, store):
-        for plane in range(planes):
-            for tile in range(wt + 1):
+    every = list(range(wt + 1))
+    before = [tile for tile in every if tile != wt - 1]
+
+    def advance(load, store, tiles, seam=None):
+        for tile in tiles:
+            for plane in range(planes):
                 is_open = load(0, plane, tile, 0) != 0.0
-                fields = [stream(load, (wt + 1, planes), slot, plane, tile, 0.0) for slot in range(Q)]
+                fields = [stream(load, (wt + 1, planes), slot, plane, tile, 0.0, seam) for slot in range(Q)]
                 result = collide_tile(fields, is_open, None, SOLID)
                 for slot in range(Q):
                     store(slot, plane, tile, result[slot])
 
-    def window(source):
+    def window(source, tiles):
         start = jnp.minimum(rows * source + 1, height - 1 - ROWS)
 
         def load(slot, plane, tile, dy):
@@ -446,7 +469,13 @@
         def store(slot, plane, tile, value):
             post2[place_of[slot], plane, tile, pl.ds(ROWS + start, ROWS), :] = value
 
-        advance(load, store)
+        def seam(slot, plane, tile, dy):
+            if tile != wt - 1:
+                return load(slot, plane, tile, dy)
+            pair = [slot in both for both in PAIRS].index(True)
+            return seams[pair, plane, pl.ds(start - dy, ROWS), :]
+
+        advance(load, store, tiles, seam)
 
     row = lax.broadcasted_iota(jnp.int32, (ROWS, LANES), 0)
     half = ROWS // 2
@@ -481,39 +510,47 @@
                 mask=(row >= half + 1) & (row < half + 3),
             )
 
-        advance(load, store)
+        advance(load, store, every)
 
     def unpack_from(step, carry):
         at = pl.ds(pl.multiple_of(lax.rem(me + step, across) * rows, ROWS), rows)
 
         def store(slot, plane, value):
-            sides[slot, plane, at, :] = value
+            if slot < Q:
+                sides[slot, plane, at, :] = value
+            else:
+                seams[slot - Q, plane, at, :] = value
 
         unpack(edges, at, store)
         return carry
 
     def unpack_ring():
         def store(slot, plane, value):
-            ring[slot, plane, wt] = value
+            if slot < Q:
+                ring[slot, plane, wt] = value
 
         unpack(ring_edges, pl.ds(0, ROWS), store)
 
     lax.fori_loop(1, across, unpack_from, 0)
     fill()
-    settle((2, 3))
-    window(me)
+    def windows(tiles):
+        def window_from(step, carry):
+            window(lax.rem(me + step, across), tiles)
+            return carry
+
+        lax.fori_loop(1, across, window_from, 0)
+
+    settle((2,))
+    windows(before)
+    settle((3,))
+    window(me, every)
     for way in range(2):
         for copy in relay(way):
             copy.wait_recv()
     unpack_ring()
     rim()
     settle((4,))
-
-    def window_from(step, carry):
-        window(lax.rem(me + step, across))
-        return carry
-
-    lax.fori_loop(1, across, window_from, 0)
+    windows([wt - 1])
 
     def sent(mine):
         for target in peers(mine):
@@ -547,20 +584,19 @@
         return post[place_of[slot], plane, tile, at - dy : at - dy + ROWS, :]
 
     copies = []
-    for slot in range(Q):
+    for start in range(0, height, ROWS):
         for plane in range(planes):
+            at = ROWS + start
             for tile in range(wt):
-                for start in range(0, height, ROWS):
-                    at = ROWS + start
-                    is_open = load(0, plane, tile, 0) != SOLID
+                is_open = load(0, plane, tile, 0) != SOLID
+                for slot in range(Q):
                     value = stream(load, (wt + 1, planes), slot, plane, tile, SOLID)
                     flow[slot, plane, start : start + ROWS, tile * LANES : (tile + 1) * LANES] = jnp.where(
                         is_open, value, 0.0
                     )
-        copies.append(pltpu.make_async_copy(flow.at[slot], out_ref.at[slot], sems.at[slot]))
-        if slot:
-            copies[slot - 1].start()
-    copies[-1].start()
+            block = (slice(None), plane, slice(start, start + ROWS))
+            copies.append(pltpu.make_async_copy(flow.at[block], out_ref.at[block], sems.at[len(copies)]))
+            copies[-1].start()
     for copy in copies:
         copy.wait()
 
@@ -571,7 +607,7 @@
     width = columns // across
     strips = columns // LANES
     wt = strips // across
-    groups = -(-count * planes * 4 // LANES)
+    groups = -(-(count + len(PAIRS)) * planes * 4 // LANES)
     tall = height + 2 * ROWS
     post2 = pl.pallas_call(
         functools.partial(kernel, across, along),
@@ -584,16 +620,18 @@
             pltpu.VMEM((count, planes, strips, rows, LANES), jnp.float32),
             pltpu.VMEM((count, planes, wt, height, LANES), jnp.float32),
             pltpu.VMEM((count, planes, height, LANES), jnp.float32),
+            pltpu.VMEM((len(PAIRS), planes, height, LANES), jnp.float32),
             pltpu.VMEM((count, planes, wt + 1, ROWS, LANES), jnp.float32),
             pltpu.VMEM((across, groups, rows, LANES), jnp.float32),
             pltpu.VMEM((groups, height, LANES), jnp.float32),
             pltpu.VMEM((groups, ROWS, LANES), jnp.float32),
-            pltpu.SemaphoreType.DMA((1 + strips,)),
+            pltpu.SemaphoreType.DMA((1 + strips * planes,)),
             pltpu.SemaphoreType.DMA((across, 5)),
             pltpu.SemaphoreType.DMA((across, 5)),
             pltpu.SemaphoreType.DMA((2, 3)),
             pltpu.SemaphoreType.DMA((2, 3)),
             pltpu.SemaphoreType.DMA((across, 3)),
+            pltpu.SemaphoreType.REGULAR,
             pltpu.SemaphoreType.REGULAR,
         ],
         compiler_params=pltpu.CompilerParams(
@@ -607,7 +645,7 @@
         out_specs=pl.BlockSpec(memory_space=pl.ANY),
         scratch_shapes=[
             pltpu.VMEM((count, planes, height, width), jnp.float32),
-            pltpu.SemaphoreType.DMA((count,)),
+            pltpu.SemaphoreType.DMA((planes * height // ROWS,)),
         ],
         compiler_params=pltpu.CompilerParams(vmem_limit_bytes=VMEM_LIMIT),
     )(post2)

time: 12.9 us -> 12.5 us (0.969)
  Pallas kernels: 12.7 us -> 12.4 us
    pallas_call x1, Pallas kernels: 11.6 us -> 11.4 us  [body(): pl.pallas_call(functools.partial(kernel, across, along), out_shape=pltpu....]
where the time goes in v3:
time: 12.5 us; the launch traced here: 12.4 us
  Pallas kernels  12.4 us (99%)
    pallas_call x1, Pallas kernels, body(): pl.pallas_call(functools.partial(kernel, across, along), out_shape=pltpu....  11.4 us
    pallas_call x1, Pallas kernels, body(): pl.pallas_call(finish, out_shape=jax.ShapeDtypeStruct((count, planes, hei...  0.95 us

profile of v3, /device:TPU:1, one launch (start us, length us, event | category | flops | bytes accessed | tf_op | source)
XLA Modules:
  0.0 12.4 jit_solution(18358954440789675518)
XLA Ops:
  0.0 11.4 %shard_map.28.post = f32[19,2,3,32,128]{4,3,2,1,0:T(8,128)S(1)} custom-call(f32[19,2,8,512]{3,2,1,0:T(8,128)} %pop_ref.1, s32[2,8,512]{2,1,0:T(8,128)} %pore_ref.1), custom_call_target="tpu_custom_call" | custom-call | tf_op jit(solution)/shard_map/pallas_call | solution.py:612
  11.4 1.0 %shard_map.29 = f32[19,2,16,256]{3,2,1,0:T(8,128)} custom-call(f32[19,2,3,32,128]{4,3,2,1,0:T(8,128)S(1)} %shard_map.28.post), custom_call_target="tpu_custom_call" | custom-call | tf_op jit(solution)/shard_map/pallas_call | solution.py:641

commit v4 on v3

--- a/solution.py
+++ b/solution.py
@@ -50,6 +50,19 @@
 PAIRS = [(s, opposite[s]) for s in range(Q) if lattice_velocity[s][0] > 0]
 
 
+def edge_layout(planes):
+    spots, group, at = [], 0, 0
+    for field in range(Q + len(PAIRS)):
+        dx = lattice_velocity[order[field]][0] if field < Q else 0
+        left, right = 1 + (dx > 0), 1 + (dx < 0)
+        for _ in range(planes):
+            if at + left + right > LANES:
+                group, at = group + 1, 0
+            spots.append((group, at + left, left, right))
+            at += left + right
+    return spots, group + 1
+
+
 def total(values):
     return functools.reduce(lambda x, y: x + y, values)
 
@@ -111,15 +124,14 @@
 
 
 def kernel(
-    across, along, pop_ref, pore_ref, post2,
+    across, along, pop_ref, pore_ref, post2, done,
     raw, voxels, box, post, sides, seams, ring, packs, edges, ring_edges,
     load_sem, n_send, n_recv, h_send, h_recv, w_send, go, ready,
 ):
     _, planes, strips, rows, _ = box.shape
     wt = strips // across
     height = across * rows
-    groups = edges.shape[0]
-    per_group = LANES // 4
+    spots, groups = edge_layout(planes)
     slabs = Q * planes
     me = lax.axis_index("px")
     here = lax.axis_index("py")
@@ -133,13 +145,15 @@
     load_pore = pltpu.make_async_copy(pore_ref, voxels, load_sem.at[0])
     load_pore.start()
 
+    own_load = (across - 1) * wt * planes
+
     def load_tile(step, k, plane):
         tile = lax.rem(me + step, across) * wt + k
         cols = pl.ds(pl.multiple_of(tile * LANES, LANES), LANES)
         return pltpu.make_async_copy(
             pop_ref.at[:, plane, :, cols],
             raw.at[:, plane, tile],
-            load_sem.at[1 + ((step - 1) * wt + k) * planes + plane],
+            load_sem.at[1 + (((step - 1) * wt + k) * planes + plane if step < across else own_load)],
         )
 
     halves = [(k, plane) for k in range(wt) for plane in range(planes)]
@@ -223,8 +237,8 @@
             return pltpu.make_async_remote_copy(
                 src_ref=box.at[:, plane, target * wt + k, low:high, :],
                 dst_ref=post.at[:, plane, k, source * rows + low : source * rows + high, :],
-                send_sem=n_send.at[target, n],
-                recv_sem=n_recv.at[source, n],
+                send_sem=n_send.at[(target - source) % across - 1, min(n, 3)],
+                recv_sem=n_recv.at[(target - source) % across - 1, n],
                 device_id=(target, here),
                 device_id_type=MESH,
             )
@@ -239,8 +253,8 @@
         return pltpu.make_async_remote_copy(
             src_ref=src,
             dst_ref=dst,
-            send_sem=n_send.at[target, n],
-            recv_sem=n_recv.at[source, n],
+            send_sem=n_send.at[(target - source) % across - 1, min(n, 3)],
+            recv_sem=n_recv.at[(target - source) % across - 1, n],
             device_id=(target, here),
             device_id_type=MESH,
         )
@@ -266,8 +280,8 @@
             pltpu.make_async_remote_copy(
                 src_ref=src,
                 dst_ref=dst,
-                send_sem=h_send.at[way, n],
-                recv_sem=h_recv.at[way, n],
+                send_sem=h_send.at[way, n // 2],
+                recv_sem=h_recv.at[way, n // 2],
                 device_id=(me, to),
                 device_id_type=MESH,
             )
@@ -301,8 +315,8 @@
             pltpu.make_async_remote_copy(
                 src_ref=src,
                 dst_ref=dst,
-                send_sem=w_send.at[target, n],
-                recv_sem=h_recv.at[1, n],
+                send_sem=w_send.at[n // 2],
+                recv_sem=h_recv.at[1, n // 2],
                 device_id=(target, 0),
                 device_id_type=MESH,
             )
@@ -330,8 +344,9 @@
 
             on_each(begin_outer)
     send_direct(range(across - 1), (0, 1))
+    own = raw.at[:, :, pl.ds(me * wt, wt)]
+    pltpu.make_async_copy(own, own, load_sem.at[1 + own_load]).wait()
     for k, plane in halves:
-        load_tile(across, k, plane).wait()
         collide_strip(me * wt + k, plane, k)
     send_direct((across - 1,), (0, 1))
 
@@ -341,31 +356,27 @@
         first = lax.rem((target + 1) * wt, strips)
         last = lax.rem(target * wt + strips - 1, strips)
         own_at = pl.ds(pl.multiple_of(me * rows, ROWS), rows)
+        packed = [None] * groups
+        for slab, (group, at, left_of, right_of) in enumerate(spots):
+            field, plane = slab // planes, slab % planes
+            if slab < slabs:
+                edge = jnp.where(lane < LANES // 2, box[field, plane, first], box[field, plane, last])
+                if step == across:
+                    sides[field, plane, own_at, :] = edge
+            else:
+                right, left = (place_of[slot] for slot in PAIRS[field - Q])
+                tile = target * wt + wt - 1
+                edge = jnp.where(lane < LANES // 2, box[left, plane, tile], box[right, plane, tile])
+                if step == across:
+                    seams[field - Q, plane, own_at, :] = edge
+            moved = pltpu.roll(edge, at, 1)
+            if packed[group] is not None:
+                moved = jnp.where((lane >= at - left_of) & (lane < at + right_of), moved, packed[group])
+            packed[group] = moved
         for group in range(groups):
-            packed = jnp.zeros((rows, LANES), jnp.float32)
-            for place in range(per_group):
-                slab = group * per_group + place
-                if slab >= slabs + len(PAIRS) * planes:
-                    break
-                field, plane = slab // planes, slab % planes
-                if slab < slabs:
-                    edge = jnp.where(lane < LANES // 2, box[field, plane, first], box[field, plane, last])
-                    if step == across:
-                        sides[field, plane, own_at, :] = edge
-                else:
-                    right, left = (place_of[slot] for slot in PAIRS[field - Q])
-                    tile = target * wt + wt - 1
-                    edge = jnp.where(lane < LANES // 2, box[left, plane, tile], box[right, plane, tile])
-                    if step == across:
-                        seams[field - Q, plane, own_at, :] = edge
-                if place == 0:
-                    packed = edge
-                else:
-                    moved = pltpu.roll(edge, 4 * place, 1)
-                    packed = jnp.where((lane >= 4 * place - 2) & (lane < 4 * place + 2), moved, packed)
-            packs[target, group] = packed
+            packs[target, group] = packed[group]
             if step == across:
-                edges[group, own_at, :] = packed
+                edges[group, own_at, :] = packed[group]
         if step == across - 1:
             begin((1,))
 
@@ -376,7 +387,14 @@
     send_direct(range(across), (2,))
     ends = ((0, 0), (across - 1, 1))
 
-    lead = 2 if wt > 1 else 3
+    def both(sem, tiles):
+        rows_of = box.at[0 : (Q + RISE) // 2, :, 0:tiles, 0:2, :]
+        pltpu.make_async_copy(rows_of, rows_of, sem).wait()
+
+    def some_edges(sem, refs):
+        pltpu.make_async_copy(refs, refs, sem).wait()
+
+    lead = 2 if wt > 1 else 0
 
     @pl.when(odd)
     def _():
@@ -397,10 +415,8 @@
         pl.semaphore_wait(ready, jnp.where(last_row, 1, 2))
 
     def unpack(packs_of, at, store):
-        for slab in range(slabs + len(PAIRS) * planes):
-            group, place = slab // per_group, slab % per_group
-            packed = packs_of[group, at, :]
-            moved = pltpu.roll(packed, LANES - 4 * place, 1) if place else packed
+        for slab, (group, lane_at, _, _) in enumerate(spots):
+            moved = pltpu.roll(packs_of[group, at, :], LANES - lane_at, 1)
             store(slab // planes, slab % planes, moved)
 
     def pass_on(mine, source, way):
@@ -545,60 +561,103 @@
     settle((3,))
     window(me, every)
     for way in range(2):
-        for copy in relay(way):
-            copy.wait_recv()
+        both(h_recv.at[way, 0], wt)
+        some_edges(h_recv.at[way, 1], ring_edges.at[:, 0:HALO, :])
     unpack_ring()
     rim()
+
+    def own_flow():
+        for plane in range(planes):
+            for tile in range(wt):
+                def store(slot, value):
+                    done[slot, plane, :, tile * LANES : (tile + 1) * LANES] = value
+
+                flow_tile(post2, pl.multiple_of(me * rows, ROWS), plane, tile, wt + 1, store)
+
+    if across == 2:
+        own_flow()
     settle((4,))
     windows([wt - 1])
+    if across != 2:
+        own_flow()
 
     def sent(mine):
         for target in peers(mine):
-            for n in pieces:
+            for n in (0, 1, 2):
+                if n not in pieces:
+                    continue
                 if n == lead:
                     pl.when(odd)(send(mine, target, n).wait_send)
                 else:
                     send(mine, target, n).wait_send()
+            low, high = rest(mine)
+            last_tile = box.at[:, :, wt - 1 : wt, low:high, :]
+            pltpu.make_async_copy(last_tile, last_tile, n_send.at[(target - mine) % across - 1, 3]).wait()
 
     on_each(sent)
-    for copy in relay(0):
-        copy.wait_send()
+    both(h_send.at[0, 0], wt)
+    some_edges(h_send.at[0, 1], ring_edges.at[:, 0:HALO, :])
 
     @pl.when(jnp.logical_not(last_row))
     def _():
-        for copy in relay(1):
-            copy.wait_send()
+        both(h_send.at[1, 0], wt)
+        some_edges(h_send.at[1, 1], ring_edges.at[:, 0:HALO, :])
 
     @pl.when(last_strip)
     def _():
-        for target in range(across):
-            for copy in direct(target):
-                copy.wait_send()
-
-
-def finish(post, out_ref, flow, sems):
-    _, planes, height, width = flow.shape
+        both(w_send.at[0], strips)
+        some_edges(w_send.at[1], packs.at[:, :, 0:HALO, :])
+
+
+def flow_tile(post, start, plane, tile, tiles, store):
+    planes = post.shape[1]
+
+    def load(slot, plane, tile, dy):
+        return post[place_of[slot], plane, tile, pl.ds(ROWS + start - dy, ROWS), :]
+
+    is_open = load(0, plane, tile, 0) != SOLID
+    for slot in range(Q):
+        value = stream(load, (tiles, planes), slot, plane, tile, SOLID)
+        store(slot, jnp.where(is_open, value, 0.0))
+
+
+def finish(across, post, done, out_ref, flow, sems):
+    _, planes, rows, width = done.shape
     wt = width // LANES
-
-    def load(slot, plane, tile, dy):
-        return post[place_of[slot], plane, tile, at - dy : at - dy + ROWS, :]
-
-    copies = []
-    for start in range(0, height, ROWS):
+    me = lax.axis_index("px")
+
+    def own_copy():
+        at = pl.ds(pl.multiple_of(me * rows, ROWS), rows)
+        return pltpu.make_async_copy(done, out_ref.at[:, :, at, :], sems.at[0])
+
+    def copy_of(step, plane):
+        at = pl.ds(pl.multiple_of(lax.rem(me + step, across) * rows, ROWS), rows)
+        return pltpu.make_async_copy(
+            flow.at[step - 1, :, plane], out_ref.at[:, plane, at, :], sems.at[1 + (step - 1) * planes + plane]
+        )
+
+    own_copy().start()
+
+    def write(step, carry):
         for plane in range(planes):
-            at = ROWS + start
             for tile in range(wt):
-                is_open = load(0, plane, tile, 0) != SOLID
-                for slot in range(Q):
-                    value = stream(load, (wt + 1, planes), slot, plane, tile, SOLID)
-                    flow[slot, plane, start : start + ROWS, tile * LANES : (tile + 1) * LANES] = jnp.where(
-                        is_open, value, 0.0
-                    )
-            block = (slice(None), plane, slice(start, start + ROWS))
-            copies.append(pltpu.make_async_copy(flow.at[block], out_ref.at[block], sems.at[len(copies)]))
-            copies[-1].start()
-    for copy in copies:
-        copy.wait()
+                def store(slot, value):
+                    flow[step - 1, slot, plane, :, tile * LANES : (tile + 1) * LANES] = value
+
+                start = pl.multiple_of(lax.rem(me + step, across) * rows, ROWS)
+                flow_tile(post, start, plane, tile, wt + 1, store)
+            copy_of(step, plane).start()
+        return carry
+
+    lax.fori_loop(1, across, write, 0)
+    own_copy().wait()
+
+    def written(step, carry):
+        for plane in range(planes):
+            copy_of(step, plane).wait()
+        return carry
+
+    lax.fori_loop(1, across, written, 0)
 
 
 def body(across, along, populations, pore):
@@ -607,13 +666,16 @@
     width = columns // across
     strips = columns // LANES
     wt = strips // across
-    groups = -(-(count + len(PAIRS)) * planes * 4 // LANES)
+    groups = edge_layout(planes)[1]
     tall = height + 2 * ROWS
-    post2 = pl.pallas_call(
+    post2, done = pl.pallas_call(
         functools.partial(kernel, across, along),
-        out_shape=pltpu.VMEM((count, planes, wt + 1, tall, LANES), jnp.float32),
+        out_shape=(
+            pltpu.VMEM((count, planes, wt + 1, tall, LANES), jnp.float32),
+            pltpu.VMEM((count, planes, rows, width), jnp.float32),
+        ),
         in_specs=[pl.BlockSpec(memory_space=pltpu.HBM)] * 2,
-        out_specs=pl.BlockSpec(memory_space=pltpu.VMEM),
+        out_specs=[pl.BlockSpec(memory_space=pltpu.VMEM)] * 2,
         scratch_shapes=[
             pltpu.VMEM((count, planes, strips, rows, LANES), jnp.float32),
             pltpu.VMEM((planes, rows, columns), jnp.int32),
@@ -625,12 +687,12 @@
             pltpu.VMEM((across, groups, rows, LANES), jnp.float32),
             pltpu.VMEM((groups, height, LANES), jnp.float32),
             pltpu.VMEM((groups, ROWS, LANES), jnp.float32),
-            pltpu.SemaphoreType.DMA((1 + strips * planes,)),
-            pltpu.SemaphoreType.DMA((across, 5)),
-            pltpu.SemaphoreType.DMA((across, 5)),
-            pltpu.SemaphoreType.DMA((2, 3)),
-            pltpu.SemaphoreType.DMA((2, 3)),
-            pltpu.SemaphoreType.DMA((across, 3)),
+            pltpu.SemaphoreType.DMA((2 + (across - 1) * wt * planes,)),
+            pltpu.SemaphoreType.DMA((across - 1, 4)),
+            pltpu.SemaphoreType.DMA((across - 1, 5)),
+            pltpu.SemaphoreType.DMA((2, 2)),
+            pltpu.SemaphoreType.DMA((2, 2)),
+            pltpu.SemaphoreType.DMA((2,)),
             pltpu.SemaphoreType.REGULAR,
             pltpu.SemaphoreType.REGULAR,
         ],
@@ -639,16 +701,16 @@
         ),
     )(*(pltpu.with_memory_space_constraint(x, pltpu.HBM) for x in (populations, pore)))
     return pl.pallas_call(
-        finish,
+        functools.partial(finish, across),
         out_shape=jax.ShapeDtypeStruct((count, planes, height, width), jnp.float32),
-        in_specs=[pl.BlockSpec(memory_space=pltpu.VMEM)],
+        in_specs=[pl.BlockSpec(memory_space=pltpu.VMEM)] * 2,
         out_specs=pl.BlockSpec(memory_space=pl.ANY),
         scratch_shapes=[
-            pltpu.VMEM((count, planes, height, width), jnp.float32),
-            pltpu.SemaphoreType.DMA((planes * height // ROWS,)),
+            pltpu.VMEM((across - 1, count, planes, rows, width), jnp.float32),
+            pltpu.SemaphoreType.DMA((1 + (across - 1) * planes,)),
         ],
         compiler_params=pltpu.CompilerParams(vmem_limit_bytes=VMEM_LIMIT),
-    )(post2)
+    )(post2, done)
 
 
 def solution(mesh):

time: 12.5 us -> 12.2 us (0.976)
  Pallas kernels: 12.4 us -> 12 us
    pallas_call x2, Pallas kernels: 12.4 us -> 12 us  [the longest x1 11.1 us: body(): pl.pallas_call(functools.partial(kernel, across, along), out_shape=(pltpu...]
where the time goes in v4:
time: 12.2 us; the launch traced here: 12 us
  Pallas kernels  12 us (98%)
    pallas_call x1, Pallas kernels, body(): pl.pallas_call(functools.partial(kernel, across, along), out_shape=(pltpu...  11.1 us
    pallas_call x1, Pallas kernels, body(): pl.pallas_call(functools.partial(finish, across), out_shape=jax.ShapeDtyp...  0.9 us

profile of v4, /device:TPU:1, one launch (start us, length us, event | category | flops | bytes accessed | tf_op | source)
XLA Modules:
  0.0 12.0 jit_solution(1990938843961174799)
XLA Ops:
  0.0 11.1 %shard_map.28 = (f32[19,2,3,32,128]{4,3,2,1,0:T(8,128)S(1)}, f32[19,2,8,256]{3,2,1,0:T(8,128)S(1)}) custom-call(f32[19,2,8,512]{3,2,1,0:T(8,128)} %pop_ref.1, s32[2,8,512]{2,1,0:T(8,128)} %pore_ref.1), custom_call_target="tpu_custom_call" | custom-call | tf_op jit(solution)/shard_map/pallas_call | solution.py:671
  11.1 0.9 %shard_map.29 = f32[19,2,16,256]{3,2,1,0:T(8,128)} custom-call(f32[19,2,3,32,128]{4,3,2,1,0:T(8,128)S(1)} %get-tuple-element.7.post, f32[19,2,8,256]{3,2,1,0:T(8,128)S(1)} %get-tuple-element.8.done), custom_call_target="tpu_custom_call" | custom-call | tf_op jit(solution)/shard_map/pallas_call | solution.py:703

commit v5 on v4

--- a/solution.py
+++ b/solution.py
@@ -64,7 +64,10 @@
 
 
 def total(values):
-    return functools.reduce(lambda x, y: x + y, values)
+    while len(values) > 1:
+        pairs = [x + y for x, y in zip(values[::2], values[1::2])]
+        values = pairs + values[2 * len(pairs) :]
+    return values[0]
 
 
 def collide_tile(fields, is_open, guard, closed):
@@ -125,8 +128,8 @@
 
 def kernel(
     across, along, pop_ref, pore_ref, post2, done,
-    raw, voxels, box, post, sides, seams, ring, packs, edges, ring_edges,
-    load_sem, n_send, n_recv, h_send, h_recv, w_send, go, ready,
+    raw, voxels, box, post, sides, seams, ring, packs, edges, ring_edges, via,
+    load_sem, n_send, n_recv, h_send, h_recv, w_send, via_sem, go, ready, path,
 ):
     _, planes, strips, rows, _ = box.shape
     wt = strips // across
@@ -141,6 +144,9 @@
     last_row = here == along - 1
     odd = lax.rem(here, 2) == 1
     last_strip = last_row & (me == across - 1)
+    quarter = along // 4
+    short = odd & (here < quarter)
+    goes_by = odd & (here >= quarter) & (here < 2 * quarter) & (me == 0)
 
     load_pore = pltpu.make_async_copy(pore_ref, voxels, load_sem.at[0])
     load_pore.start()
@@ -180,6 +186,10 @@
         def _():
             greet(me, down)
 
+    @pl.when(short & (me == 0))
+    def _():
+        greet(0, here + quarter)
+
     @pl.when(first_row)
     def _():
         greet(me, along - 1)
@@ -191,7 +201,12 @@
     def enter():
         greeted = jnp.where(odd, 0, 2) - jnp.where(first_row, 1, 0)
         greeted = greeted + jnp.where(last_row, jnp.where(me == across - 1, across, 1), 0)
+        greeted = greeted + jnp.where(goes_by, 1, 0)
         pl.semaphore_wait(barrier, across - 1 + greeted)
+
+        @pl.when(goes_by)
+        def _():
+            pl.semaphore_signal(path, inc=1, device_id=(0, here - quarter), device_id_type=MESH)
 
         @pl.when(jnp.logical_not(odd))
         def _():
@@ -396,10 +411,47 @@
 
     lead = 2 if wt > 1 else 0
 
+    end = across - 1
+    low, high = inner(end)
+    around = pltpu.make_async_remote_copy(
+        src_ref=box.at[:, :, wt - 1 : wt, low:high, :],
+        dst_ref=via,
+        send_sem=n_send.at[(0 - end) % across - 1, 3],
+        recv_sem=via_sem.at[0],
+        device_id=(0, here + quarter),
+        device_id_type=MESH,
+    )
+    onward = pltpu.make_async_remote_copy(
+        src_ref=via,
+        dst_ref=post.at[:, :, wt - 1 : wt, end * rows + low : end * rows + high, :],
+        send_sem=via_sem.at[1],
+        recv_sem=n_recv.at[(0 - end) % across - 1, 3],
+        device_id=(0, here - quarter),
+        device_id_type=MESH,
+    )
+
+    @pl.when(short & (me == 0))
+    def _():
+        pl.semaphore_wait(path, 1)
+        pl.semaphore_signal(path, inc=1, device_id=(end, here), device_id_type=MESH)
+
+    @pl.when(short & (me == end))
+    def _():
+        pl.semaphore_wait(path, 1)
+        around.start()
+
+    def begin_late(mine):
+        for n in pieces:
+            for target in peers(mine):
+                if n == 3 and (mine, target) == (end, 0):
+                    pl.when(jnp.logical_not(short))(send(mine, target, n).start)
+                elif n >= 2:
+                    send(mine, target, n).start()
+
     @pl.when(odd)
     def _():
         pl.semaphore_wait(go, 1)
-        begin((2, 3, 4))
+        on_each(begin_late)
 
     def lead_sent(mine):
         for target in peers(mine):
@@ -556,15 +608,21 @@
 
         lax.fori_loop(1, across, window_from, 0)
 
+    @pl.when(goes_by)
+    def _():
+        around.wait_recv()
+        onward.start()
+
     settle((2,))
     windows(before)
     settle((3,))
     window(me, every)
-    for way in range(2):
-        both(h_recv.at[way, 0], wt)
-        some_edges(h_recv.at[way, 1], ring_edges.at[:, 0:HALO, :])
-    unpack_ring()
-    rim()
+    def halo():
+        for way in range(2):
+            both(h_recv.at[way, 0], wt)
+            some_edges(h_recv.at[way, 1], ring_edges.at[:, 0:HALO, :])
+        unpack_ring()
+        rim()
 
     def own_flow():
         for plane in range(planes):
@@ -574,11 +632,23 @@
 
                 flow_tile(post2, pl.multiple_of(me * rows, ROWS), plane, tile, wt + 1, store)
 
-    if across == 2:
-        own_flow()
-    settle((4,))
-    windows([wt - 1])
-    if across != 2:
+    def last_windows():
+        settle((4,))
+        windows([wt - 1])
+
+    @pl.when(odd)
+    def _():
+        halo()
+        if across == 2:
+            own_flow()
+        last_windows()
+        if across != 2:
+            own_flow()
+
+    @pl.when(jnp.logical_not(odd))
+    def _():
+        last_windows()
+        halo()
         own_flow()
 
     def sent(mine):
@@ -594,6 +664,7 @@
             last_tile = box.at[:, :, wt - 1 : wt, low:high, :]
             pltpu.make_async_copy(last_tile, last_tile, n_send.at[(target - mine) % across - 1, 3]).wait()
 
+    pl.when(goes_by)(onward.wait_send)
     on_each(sent)
     both(h_send.at[0, 0], wt)
     some_edges(h_send.at[0, 1], ring_edges.at[:, 0:HALO, :])
@@ -687,12 +758,15 @@
             pltpu.VMEM((across, groups, rows, LANES), jnp.float32),
             pltpu.VMEM((groups, height, LANES), jnp.float32),
             pltpu.VMEM((groups, ROWS, LANES), jnp.float32),
+            pltpu.VMEM((count, planes, 1, HALO, LANES), jnp.float32),
             pltpu.SemaphoreType.DMA((2 + (across - 1) * wt * planes,)),
             pltpu.SemaphoreType.DMA((across - 1, 4)),
             pltpu.SemaphoreType.DMA((across - 1, 5)),
             pltpu.SemaphoreType.DMA((2, 2)),
             pltpu.SemaphoreType.DMA((2, 2)),
             pltpu.SemaphoreType.DMA((2,)),
+            pltpu.SemaphoreType.DMA((2,)),
+            pltpu.SemaphoreType.REGULAR,
             pltpu.SemaphoreType.REGULAR,
             pltpu.SemaphoreType.REGULAR,
         ],

time: 12.2 us -> 12 us (0.984)
  Pallas kernels: 12 us -> 11.8 us
    pallas_call x1, Pallas kernels: 11.1 us -> 10.9 us  [body(): pl.pallas_call(functools.partial(kernel, across, along), out_shape=(pltpu...]
where the time goes in v5:
time: 12 us; the launch traced here: 11.8 us
  Pallas kernels  11.8 us (98%)
    pallas_call x1, Pallas kernels, body(): pl.pallas_call(functools.partial(kernel, across, along), out_shape=(pltpu...  10.9 us
    pallas_call x1, Pallas kernels, body(): pl.pallas_call(functools.partial(finish, across), out_shape=jax.ShapeDtyp...  0.9 us

profile of v5, /device:TPU:1, one launch (start us, length us, event | category | flops | bytes accessed | tf_op | source)
XLA Modules:
  0.0 11.8 jit_solution(14830925273538411038)
XLA Ops:
  0.0 10.9 %shard_map.28 = (f32[19,2,3,32,128]{4,3,2,1,0:T(8,128)S(1)}, f32[19,2,8,256]{3,2,1,0:T(8,128)S(1)}) custom-call(f32[19,2,8,512]{3,2,1,0:T(8,128)} %pop_ref.1, s32[2,8,512]{2,1,0:T(8,128)} %pore_ref.1), custom_call_target="tpu_custom_call" | custom-call | tf_op jit(solution)/shard_map/pallas_call | solution.py:742
  11.0 0.9 %shard_map.29 = f32[19,2,16,256]{3,2,1,0:T(8,128)} custom-call(f32[19,2,3,32,128]{4,3,2,1,0:T(8,128)S(1)} %get-tuple-element.7.post, f32[19,2,8,256]{3,2,1,0:T(8,128)S(1)} %get-tuple-element.8.done), custom_call_target="tpu_custom_call" | custom-call | tf_op jit(solution)/shard_map/pallas_call | solution.py:777

commit v6 on v5

--- a/solution.py
+++ b/solution.py
@@ -144,6 +144,7 @@
     last_row = here == along - 1
     odd = lax.rem(here, 2) == 1
     last_strip = last_row & (me == across - 1)
+    end = across - 1
     quarter = along // 4
     short = odd & (here < quarter)
     goes_by = odd & (here >= quarter) & (here < 2 * quarter) & (me == 0)
@@ -239,9 +240,6 @@
     def inner(source):
         return (0, HALO) if source == across - 1 else (rows - HALO, rows)
 
-    def rest(source):
-        return (0, rows - HALO) if source == across - 1 else (HALO, rows)
-
     def middle(source):
         return (HALO, rows - HALO)
 
@@ -252,29 +250,29 @@
             return pltpu.make_async_remote_copy(
                 src_ref=box.at[:, plane, target * wt + k, low:high, :],
                 dst_ref=post.at[:, plane, k, source * rows + low : source * rows + high, :],
-                send_sem=n_send.at[(target - source) % across - 1, min(n, 3)],
-                recv_sem=n_recv.at[(target - source) % across - 1, n],
+                send_sem=n_send.at[(target - source) % across - 1, (0, 1, 2, 2, 3, 3)[n]],
+                recv_sem=n_recv.at[(target - source) % across - 1, (0, 1, 2, 2, 3, 4)[n]],
                 device_id=(target, here),
                 device_id_type=MESH,
             )
         if n == 1:
             src, dst = packs.at[target], edges.at[:, source * rows : (source + 1) * rows, :]
         else:
-            low, high = (outer, None, rest, inner, middle)[n](source)
-            first, last = ((0, wt), None, (0, wt - 1), (wt - 1, wt), (wt - 1, wt))[n]
+            low, high = (outer, None, inner, inner, middle, middle)[n](source)
+            first, last = ((0, wt), None, (0, wt - 1), (wt - 1, wt))[n if n < 4 else n - 2]
             src = box.at[:, :, target * wt + first : target * wt + last, low:high, :]
             start = source * rows
             dst = post.at[:, :, first:last, start + low : start + high, :]
         return pltpu.make_async_remote_copy(
             src_ref=src,
             dst_ref=dst,
-            send_sem=n_send.at[(target - source) % across - 1, min(n, 3)],
-            recv_sem=n_recv.at[(target - source) % across - 1, n],
+            send_sem=n_send.at[(target - source) % across - 1, (0, 1, 2, 2, 3, 3)[n]],
+            recv_sem=n_recv.at[(target - source) % across - 1, (0, 1, 2, 2, 3, 4)[n]],
             device_id=(target, here),
             device_id_type=MESH,
         )
 
-    pieces = [0, 1, 2, 3, 4] if wt > 1 else [0, 1, 3, 4]
+    pieces = [0, 1, 2, 3, 4, 5] if wt > 1 else [0, 1, 3, 5]
 
     def relay(way):
         if way == 0:
@@ -397,10 +395,9 @@
 
             @pl.when(jnp.logical_not(odd))
             def _():
-                begin((2, 3, 4))
+                begin((2, 3, 4, 5))
 
     send_direct(range(across), (2,))
-    ends = ((0, 0), (across - 1, 1))
 
     def both(sem, tiles):
         rows_of = box.at[0 : (Q + RISE) // 2, :, 0:tiles, 0:2, :]
@@ -409,14 +406,17 @@
     def some_edges(sem, refs):
         pltpu.make_async_copy(refs, refs, sem).wait()
 
-    lead = 2 if wt > 1 else 0
-
-    end = across - 1
+    def all_of(sem, part, mine):
+        low, high = part(mine)
+        refs = box.at[:, :, 0:wt, low:high, :]
+        pltpu.make_async_copy(refs, refs, sem).wait()
+
+
     low, high = inner(end)
     around = pltpu.make_async_remote_copy(
         src_ref=box.at[:, :, wt - 1 : wt, low:high, :],
         dst_ref=via,
-        send_sem=n_send.at[(0 - end) % across - 1, 3],
+        send_sem=n_send.at[(0 - end) % across - 1, 2],
         recv_sem=via_sem.at[0],
         device_id=(0, here + quarter),
         device_id_type=MESH,
@@ -425,7 +425,7 @@
         src_ref=via,
         dst_ref=post.at[:, :, wt - 1 : wt, end * rows + low : end * rows + high, :],
         send_sem=via_sem.at[1],
-        recv_sem=n_recv.at[(0 - end) % across - 1, 3],
+        recv_sem=n_recv.at[(0 - end) % across - 1, 2],
         device_id=(0, here - quarter),
         device_id_type=MESH,
     )
@@ -434,6 +434,22 @@
     def _():
         pl.semaphore_wait(path, 1)
         pl.semaphore_signal(path, inc=1, device_id=(end, here), device_id_type=MESH)
+
+    @pl.when(odd)
+    def _():
+        pl.semaphore_wait(ready, jnp.where(last_row, 1, 2))
+
+    def start_relay(way):
+        for copy in relay(way):
+            copy.start()
+
+    @pl.when((me == 0) & jnp.logical_not(first_row))
+    def _():
+        start_relay(0)
+
+    @pl.when((me == end) & jnp.logical_not(last_row))
+    def _():
+        start_relay(1)
 
     @pl.when(short & (me == end))
     def _():
@@ -455,61 +471,48 @@
 
     def lead_sent(mine):
         for target in peers(mine):
-            send(mine, target, lead).wait_send()
+            all_of(n_send.at[(target - mine) % across - 1, 2], inner, mine)
 
     @pl.when(jnp.logical_not(odd))
     def _():
         on_each(lead_sent)
         pl.semaphore_signal(go, inc=1, device_id=(me, down), device_id_type=MESH)
-
-    @pl.when(odd)
-    def _():
-        pl.semaphore_wait(ready, jnp.where(last_row, 1, 2))
 
     def unpack(packs_of, at, store):
         for slab, (group, lane_at, _, _) in enumerate(spots):
             moved = pltpu.roll(packs_of[group, at, :], LANES - lane_at, 1)
             store(slab // planes, slab % planes, moved)
 
-    def pass_on(mine, source, way):
-        if source != mine:
-            send(source, mine, 0).wait_recv()
-            send(source, mine, 1).wait_recv()
-
-        def start():
-            for copy in relay(way):
-                copy.start()
-
-        if way:
-            pl.when(jnp.logical_not(last_row))(start)
-        else:
-            start()
+    def take_outer(source, mine):
+        send(source, mine, 0).wait_recv()
+        send(source, mine, 1).wait_recv()
 
     def relays(mine):
+        if mine != end:
+            take_outer(end, mine)
+            pl.when(jnp.logical_not(last_row))(functools.partial(start_relay, 1))
+        if mine != 0:
+            take_outer(0, mine)
+            pl.when(jnp.logical_not(first_row))(functools.partial(start_relay, 0))
+
         @pl.when(first_row)
         def _():
-            pass_on(mine, across - 1, 1)
             pl.semaphore_wait(ready, 1)
-            pass_on(mine, 0, 0)
-
-        @pl.when(jnp.logical_not(first_row))
-        def _():
-            for source, way in sorted(ends, key=lambda end: end[0] != mine):
-                pass_on(mine, source, way)
+            start_relay(0)
 
         for source in peers(mine):
-            if source not in (0, across - 1):
-                send(source, mine, 0).wait_recv()
-                send(source, mine, 1).wait_recv()
+            if source not in (0, end):
+                take_outer(source, mine)
 
     on_each(relays)
 
-    def settle(wanted):
+    def settle(n):
         def action(mine):
             for source in peers(mine):
-                for n in pieces:
-                    if n in wanted:
-                        send(source, mine, n).wait_recv()
+                if n == 2:
+                    all_of(n_recv.at[(mine - source) % across - 1, 2], inner, source)
+                elif n + 1 in pieces:
+                    send(source, mine, n + 1).wait_recv()
 
         on_each(action)
 
@@ -613,10 +616,6 @@
         around.wait_recv()
         onward.start()
 
-    settle((2,))
-    windows(before)
-    settle((3,))
-    window(me, every)
     def halo():
         for way in range(2):
             both(h_recv.at[way, 0], wt)
@@ -632,37 +631,44 @@
 
                 flow_tile(post2, pl.multiple_of(me * rows, ROWS), plane, tile, wt + 1, store)
 
+    def own_window():
+        settle(2)
+        window(me, every)
+
+    def first_windows():
+        settle(3)
+        windows(before)
+
     def last_windows():
-        settle((4,))
+        settle(4)
         windows([wt - 1])
 
     @pl.when(odd)
     def _():
         halo()
+        own_window()
         if across == 2:
             own_flow()
+        first_windows()
         last_windows()
         if across != 2:
             own_flow()
 
     @pl.when(jnp.logical_not(odd))
     def _():
+        own_window()
+        first_windows()
         last_windows()
         halo()
         own_flow()
 
     def sent(mine):
         for target in peers(mine):
-            for n in (0, 1, 2):
-                if n not in pieces:
-                    continue
-                if n == lead:
-                    pl.when(odd)(send(mine, target, n).wait_send)
-                else:
-                    send(mine, target, n).wait_send()
-            low, high = rest(mine)
-            last_tile = box.at[:, :, wt - 1 : wt, low:high, :]
-            pltpu.make_async_copy(last_tile, last_tile, n_send.at[(target - mine) % across - 1, 3]).wait()
+            send(mine, target, 0).wait_send()
+            send(mine, target, 1).wait_send()
+            sem = (target - mine) % across - 1
+            pl.when(odd)(functools.partial(all_of, n_send.at[sem, 2], inner, mine))
+            all_of(n_send.at[sem, 3], middle, mine)
 
     pl.when(goes_by)(onward.wait_send)
     on_each(sent)

time: 12 us -> 11.8 us (0.983)
  Pallas kernels: 11.8 us -> 11.6 us
    pallas_call x1, Pallas kernels: 10.9 us -> 10.7 us  [body(): pl.pallas_call(functools.partial(kernel, across, along), out_shape=(pltpu...]
where the time goes in v6:
time: 11.8 us; the launch traced here: 11.6 us
  Pallas kernels  11.6 us (98%)
    pallas_call x1, Pallas kernels, body(): pl.pallas_call(functools.partial(kernel, across, along), out_shape=(pltpu...  10.7 us
    pallas_call x1, Pallas kernels, body(): pl.pallas_call(functools.partial(finish, across), out_shape=jax.ShapeDtyp...  0.9 us

profile of v6, /device:TPU:1, one launch (start us, length us, event | category | flops | bytes accessed | tf_op | source)
XLA Modules:
  0.0 11.6 jit_solution(15572126639006356737)
XLA Ops:
  0.0 10.7 %shard_map.28 = (f32[19,2,3,32,128]{4,3,2,1,0:T(8,128)S(1)}, f32[19,2,8,256]{3,2,1,0:T(8,128)S(1)}) custom-call(f32[19,2,8,512]{3,2,1,0:T(8,128)} %pop_ref.1, s32[2,8,512]{2,1,0:T(8,128)} %pore_ref.1), custom_call_target="tpu_custom_call" | custom-call | tf_op jit(solution)/shard_map/pallas_call | solution.py:748
  10.7 0.9 %shard_map.29 = f32[19,2,16,256]{3,2,1,0:T(8,128)} custom-call(f32[19,2,3,32,128]{4,3,2,1,0:T(8,128)S(1)} %get-tuple-element.7.post, f32[19,2,8,256]{3,2,1,0:T(8,128)S(1)} %get-tuple-element.8.done), custom_call_target="tpu_custom_call" | custom-call | tf_op jit(solution)/shard_map/pallas_call | solution.py:783

commit v7 on v6

--- a/solution.py
+++ b/solution.py
@@ -136,6 +136,21 @@
     height = across * rows
     spots, groups = edge_layout(planes)
     slabs = Q * planes
+
+    def load_tile(tile, plane, cols):
+        return pltpu.make_async_copy(
+            pop_ref.at[:, plane, :, cols],
+            raw.at[:, plane, tile],
+            load_sem.at[1 + tile * planes + plane],
+        )
+
+    load_pore = pltpu.make_async_copy(pore_ref, voxels, load_sem.at[0])
+    for tile in range(strips):
+        for plane in range(planes):
+            load_tile(tile, plane, slice(tile * LANES, (tile + 1) * LANES)).start()
+        if tile == 0:
+            load_pore.start()
+
     me = lax.axis_index("px")
     here = lax.axis_index("py")
     up = lax.rem(here + along - 1, along)
@@ -149,24 +164,10 @@
     short = odd & (here < quarter)
     goes_by = odd & (here >= quarter) & (here < 2 * quarter) & (me == 0)
 
-    load_pore = pltpu.make_async_copy(pore_ref, voxels, load_sem.at[0])
-    load_pore.start()
-
-    own_load = (across - 1) * wt * planes
-
-    def load_tile(step, k, plane):
-        tile = lax.rem(me + step, across) * wt + k
-        cols = pl.ds(pl.multiple_of(tile * LANES, LANES), LANES)
-        return pltpu.make_async_copy(
-            pop_ref.at[:, plane, :, cols],
-            raw.at[:, plane, tile],
-            load_sem.at[1 + (((step - 1) * wt + k) * planes + plane if step < across else own_load)],
-        )
-
     halves = [(k, plane) for k in range(wt) for plane in range(planes)]
-    for step in range(1, across + 1):
-        for k, plane in halves:
-            load_tile(step, k, plane).start()
+
+    def loaded(tile, plane):
+        load_tile(tile, plane, slice(0, LANES)).wait()
 
     barrier = pltpu.get_barrier_semaphore()
 
@@ -205,6 +206,7 @@
         greeted = greeted + jnp.where(goes_by, 1, 0)
         pl.semaphore_wait(barrier, across - 1 + greeted)
 
+    def answers():
         @pl.when(goes_by)
         def _():
             pl.semaphore_signal(path, inc=1, device_id=(0, here - quarter), device_id_type=MESH)
@@ -347,8 +349,9 @@
 
     for step in range(1, across):
         for k, plane in halves:
-            load_tile(step, k, plane).wait()
-            collide_strip(lax.rem(me + step, across) * wt + k, plane, None)
+            tile = lax.rem(me + step, across) * wt + k
+            loaded(tile, plane)
+            collide_strip(tile, plane, None)
             if step == 1 and (k, plane) == (0, 0):
                 enter()
 
@@ -356,9 +359,11 @@
                 send(mine, (mine + step) % across, 0, (k, plane)).start()
 
             on_each(begin_outer)
+            if step == 1 and (k, plane) == (0, 0):
+                answers()
     send_direct(range(across - 1), (0, 1))
-    own = raw.at[:, :, pl.ds(me * wt, wt)]
-    pltpu.make_async_copy(own, own, load_sem.at[1 + own_load]).wait()
+    for k, plane in halves:
+        loaded(me * wt + k, plane)
     for k, plane in halves:
         collide_strip(me * wt + k, plane, k)
     send_direct((across - 1,), (0, 1))
@@ -392,12 +397,13 @@
                 edges[group, own_at, :] = packed[group]
         if step == across - 1:
             begin((1,))
+            send_direct(range(across - 1), (2,))
 
             @pl.when(jnp.logical_not(odd))
             def _():
                 begin((2, 3, 4, 5))
 
-    send_direct(range(across), (2,))
+    send_direct((across - 1,), (2,))
 
     def both(sem, tiles):
         rows_of = box.at[0 : (Q + RISE) // 2, :, 0:tiles, 0:2, :]
@@ -643,25 +649,6 @@
         settle(4)
         windows([wt - 1])
 
-    @pl.when(odd)
-    def _():
-        halo()
-        own_window()
-        if across == 2:
-            own_flow()
-        first_windows()
-        last_windows()
-        if across != 2:
-            own_flow()
-
-    @pl.when(jnp.logical_not(odd))
-    def _():
-        own_window()
-        first_windows()
-        last_windows()
-        halo()
-        own_flow()
-
     def sent(mine):
         for target in peers(mine):
             send(mine, target, 0).wait_send()
@@ -670,20 +657,42 @@
             pl.when(odd)(functools.partial(all_of, n_send.at[sem, 2], inner, mine))
             all_of(n_send.at[sem, 3], middle, mine)
 
-    pl.when(goes_by)(onward.wait_send)
-    on_each(sent)
-    both(h_send.at[0, 0], wt)
-    some_edges(h_send.at[0, 1], ring_edges.at[:, 0:HALO, :])
-
-    @pl.when(jnp.logical_not(last_row))
-    def _():
-        both(h_send.at[1, 0], wt)
-        some_edges(h_send.at[1, 1], ring_edges.at[:, 0:HALO, :])
-
-    @pl.when(last_strip)
-    def _():
-        both(w_send.at[0], strips)
-        some_edges(w_send.at[1], packs.at[:, :, 0:HALO, :])
+    def all_sent():
+        pl.when(goes_by)(onward.wait_send)
+        on_each(sent)
+        both(h_send.at[0, 0], wt)
+        some_edges(h_send.at[0, 1], ring_edges.at[:, 0:HALO, :])
+
+        @pl.when(jnp.logical_not(last_row))
+        def _():
+            both(h_send.at[1, 0], wt)
+            some_edges(h_send.at[1, 1], ring_edges.at[:, 0:HALO, :])
+
+        @pl.when(last_strip)
+        def _():
+            both(w_send.at[0], strips)
+            some_edges(w_send.at[1], packs.at[:, :, 0:HALO, :])
+
+    @pl.when(odd)
+    def _():
+        halo()
+        own_window()
+        if across == 2:
+            own_flow()
+        first_windows()
+        all_sent()
+        last_windows()
+        if across != 2:
+            own_flow()
+
+    @pl.when(jnp.logical_not(odd))
+    def _():
+        own_window()
+        first_windows()
+        last_windows()
+        all_sent()
+        halo()
+        own_flow()
 
 
 def flow_tile(post, start, plane, tile, tiles, store):
@@ -765,7 +774,7 @@
             pltpu.VMEM((groups, height, LANES), jnp.float32),
             pltpu.VMEM((groups, ROWS, LANES), jnp.float32),
             pltpu.VMEM((count, planes, 1, HALO, LANES), jnp.float32),
-            pltpu.SemaphoreType.DMA((2 + (across - 1) * wt * planes,)),
+            pltpu.SemaphoreType.DMA((1 + strips * planes,)),
             pltpu.SemaphoreType.DMA((across - 1, 4)),
             pltpu.SemaphoreType.DMA((across - 1, 5)),
             pltpu.SemaphoreType.DMA((2, 2)),

time: 11.8 us -> 11.8 us (level)
  no operation moved by 1% of the time
where the time goes in v7:
time: 11.8 us; the launch traced here: 11.6 us
  Pallas kernels  11.6 us (98%)
    pallas_call x1, Pallas kernels, body(): pl.pallas_call(functools.partial(kernel, across, along), out_shape=(pltpu...  10.7 us
    pallas_call x1, Pallas kernels, body(): pl.pallas_call(functools.partial(finish, across), out_shape=jax.ShapeDtyp...  0.9 us

profile of v7, /device:TPU:1, one launch (start us, length us, event | category | flops | bytes accessed | tf_op | source)
XLA Modules:
  0.0 11.6 jit_solution(11495003365507018039)
XLA Ops:
  0.0 10.7 %shard_map.28 = (f32[19,2,3,32,128]{4,3,2,1,0:T(8,128)S(1)}, f32[19,2,8,256]{3,2,1,0:T(8,128)S(1)}) custom-call(f32[19,2,8,512]{3,2,1,0:T(8,128)} %pop_ref.1, s32[2,8,512]{2,1,0:T(8,128)} %pore_ref.1), custom_call_target="tpu_custom_call" | custom-call | tf_op jit(solution)/shard_map/pallas_call | solution.py:757
  10.7 0.9 %shard_map.29 = f32[19,2,16,256]{3,2,1,0:T(8,128)} custom-call(f32[19,2,3,32,128]{4,3,2,1,0:T(8,128)S(1)} %get-tuple-element.7.post, f32[19,2,8,256]{3,2,1,0:T(8,128)S(1)} %get-tuple-element.8.done), custom_call_target="tpu_custom_call" | custom-call | tf_op jit(solution)/shard_map/pallas_call | solution.py:792

commit v8 on v7

--- a/solution.py
+++ b/solution.py
@@ -129,7 +129,7 @@
 def kernel(
     across, along, pop_ref, pore_ref, post2, done,
     raw, voxels, box, post, sides, seams, ring, packs, edges, ring_edges, via,
-    load_sem, n_send, n_recv, h_send, h_recv, w_send, via_sem, go, ready, path,
+    load_sem, n_send, n_recv, h_send, h_recv, via_sem, go, ready, path,
 ):
     _, planes, strips, rows, _ = box.shape
     wt = strips // across
@@ -330,7 +330,7 @@
             pltpu.make_async_remote_copy(
                 src_ref=src,
                 dst_ref=dst,
-                send_sem=w_send.at[n // 2],
+                send_sem=h_send.at[1, n // 2],
                 recv_sem=h_recv.at[1, n // 2],
                 device_id=(target, 0),
                 device_id_type=MESH,
@@ -670,8 +670,8 @@
 
         @pl.when(last_strip)
         def _():
-            both(w_send.at[0], strips)
-            some_edges(w_send.at[1], packs.at[:, :, 0:HALO, :])
+            both(h_send.at[1, 0], strips)
+            some_edges(h_send.at[1, 1], packs.at[:, :, 0:HALO, :])
 
     @pl.when(odd)
     def _():
@@ -780,7 +780,6 @@
             pltpu.SemaphoreType.DMA((2, 2)),
             pltpu.SemaphoreType.DMA((2, 2)),
             pltpu.SemaphoreType.DMA((2,)),
-            pltpu.SemaphoreType.DMA((2,)),
             pltpu.SemaphoreType.REGULAR,
             pltpu.SemaphoreType.REGULAR,
             pltpu.SemaphoreType.REGULAR,

time: 11.8 us -> 11.8 us (level)
  no operation moved by 1% of the time
where the time goes in v8:
time: 11.8 us; the launch traced here: 11.6 us
  Pallas kernels  11.6 us (98%)
    pallas_call x1, Pallas kernels, body(): pl.pallas_call(functools.partial(kernel, across, along), out_shape=(pltpu...  10.7 us
    pallas_call x1, Pallas kernels, body(): pl.pallas_call(functools.partial(finish, across), out_shape=jax.ShapeDtyp...  0.9 us

profile of v8, /device:TPU:1, one launch (start us, length us, event | category | flops | bytes accessed | tf_op | source)
XLA Modules:
  0.0 11.6 jit_solution(10966992550972813229)
XLA Ops:
  0.0 10.7 %shard_map.28 = (f32[19,2,3,32,128]{4,3,2,1,0:T(8,128)S(1)}, f32[19,2,8,256]{3,2,1,0:T(8,128)S(1)}) custom-call(f32[19,2,8,512]{3,2,1,0:T(8,128)} %pop_ref.1, s32[2,8,512]{2,1,0:T(8,128)} %pore_ref.1), custom_call_target="tpu_custom_call" | custom-call | tf_op jit(solution)/shard_map/pallas_call | solution.py:757
  10.7 0.9 %shard_map.29 = f32[19,2,16,256]{3,2,1,0:T(8,128)} custom-call(f32[19,2,3,32,128]{4,3,2,1,0:T(8,128)S(1)} %get-tuple-element.7.post, f32[19,2,8,256]{3,2,1,0:T(8,128)S(1)} %get-tuple-element.8.done), custom_call_target="tpu_custom_call" | custom-call | tf_op jit(solution)/shard_map/pallas_call | solution.py:791
